TPU v7x, 128 devices: a whole 4x4x4 slice. The times are simulated.
128 devices in a mesh: seq: 16 (over z_hi, y, core), tensor: 8 (over z_lo, x).
Axes of the slice: x: 4, y: 4, z: 4 (z_hi: 2, z_lo: 2; z = z_hi * 2 + z_lo), core: 2. Of those that a mesh axis runs over, the one named last changes fastest.
Arguments:
- tokens: bfloat16 [11520, 1536], P('seq'), may hold values from -6 to 6
- norm_gain: float32 [1536], replicated, may hold values from 0.1 to 1.9
- w_qkv: bfloat16 [1536, 3, 1536], P(None, None, 'tensor'), may hold values from -8 to 8
- w_out: bfloat16 [1536, 1536], P('tensor'), may hold values from -0.15625 to 0.15625
- post_gain: float32 [1536], replicated, may hold values from 0.1 to 1.9
- w_up: bfloat16 [1536, 6144], P(None, 'tensor'), may hold values from -0.15625 to 0.15625
- w_down: bfloat16 [6144, 1536], P('tensor'), may hold values from -0.078125 to 0.078125
Outputs:
- layer_out: bfloat16 [11520, 1536], P('seq')
All inputs are finite; a program needn't handle non-finite values.
Results may differ from a plain program's by a relative error of at most 0.015.
Values may be sent and summed in bfloat16 or wider, within the bound.
A program may use at most 128 MiB of HBM per device.

v0:
```python
import functools
import jax
import jax.numpy as jnp
from jax import lax
from jax.experimental import pallas as pl
from jax.experimental.pallas import tpu as pltpu
from jax.sharding import PartitionSpec as P

HD = 48
LOG2E = 1.4426950408889634


def layer_norm(values, gain):
    mean = jnp.mean(values, axis=-1, keepdims=True)
    centred = values - mean
    var = jnp.mean(centred * centred, axis=-1, keepdims=True)
    return centred * lax.rsqrt(var + 1e-05) * gain


def attend_kernel(q_ref, k_ref, v_ref, out_ref, key_rows, values):
    blocks, width, rows = k_ref.shape

    @pl.when(pl.program_id(0) == 0)
    def _():
        for c in range(blocks):
            key_rows[c] = k_ref[c].T
            values[c, :width] = v_ref[c]
            values[c, width:] = jnp.ones((values.shape[1] - width, rows), values.dtype)

    query = q_ref[0]
    peak = jnp.full((1, query.shape[1]), -1e30, jnp.float32)
    accum = jnp.zeros((values.shape[1], query.shape[1]), jnp.float32)
    for c in range(blocks):
        scores = jnp.dot(key_rows[c], query, preferred_element_type=jnp.float32)
        fresh = jnp.maximum(peak, jnp.max(scores, axis=0, keepdims=True))
        weights = jnp.exp2(scores - fresh).astype(jnp.bfloat16)
        accum = accum * jnp.exp2(peak - fresh) + jnp.dot(
            values[c], weights, preferred_element_type=jnp.float32
        )
        peak = fresh
    out_ref[0] = (accum[:width] / accum[width : width + 1]).astype(out_ref.dtype)


def attend(query, key, value):
    blocks, width, rows = key.shape
    qblocks, _, qrows = query.shape
    flops = 4 * qblocks * qrows * blocks * rows * width
    whole = lambda i: (0, 0, 0)
    return pl.pallas_call(
        attend_kernel,
        grid=(qblocks,),
        in_specs=[
            pl.BlockSpec((1, width, qrows), lambda i: (i, 0, 0)),
            pl.BlockSpec((blocks, width, rows), whole),
            pl.BlockSpec((blocks, width, rows), whole),
        ],
        out_specs=pl.BlockSpec((1, width, qrows), lambda i: (i, 0, 0)),
        out_shape=jax.ShapeDtypeStruct(query.shape, jnp.bfloat16),
        scratch_shapes=[
            pltpu.VMEM((blocks, rows, width), jnp.bfloat16),
            pltpu.VMEM((blocks, width + 16, rows), jnp.bfloat16),
        ],
        cost_estimate=pl.CostEstimate(flops=flops * 8, bytes_accessed=8 << 20, transcendentals=0),
        compiler_params=pltpu.CompilerParams(vmem_limit_bytes=56 << 20),
    )(query, key, value)


def per_device(n_seq, n_tensor, tokens, norm_gain, w_qkv, w_out, post_gain, w_up, w_down):
    rows, model = tokens.shape
    span = w_qkv.shape[2]
    heads = span // HD
    share = n_seq // heads
    part = rows // n_tensor
    me = lax.axis_index("tensor")

    w_out_all = lax.all_gather(w_out, "tensor", axis=0, tiled=True)

    base = tokens.astype(jnp.float32)
    normed = layer_norm(base, norm_gain).astype(jnp.bfloat16)
    qkv = lax.dot_general(
        w_qkv.reshape(model, -1), normed, (((0,), (1,)), ((), ())), preferred_element_type=jnp.float32
    ).reshape(3, heads, HD, rows)
    query = (qkv[0] * (LOG2E / HD**0.5)).astype(jnp.bfloat16)
    key, value = qkv[1].astype(jnp.bfloat16), qkv[2].astype(jnp.bfloat16)
    if share > 1:
        query = query.reshape(heads, HD, share, rows // share).transpose(0, 2, 1, 3)
        query = query.reshape(n_seq, HD, rows // share)
        key = jnp.repeat(key, share, axis=0)
        value = jnp.repeat(value, share, axis=0)
        send = lambda x: lax.all_to_all(x, "seq", 0, 0, tiled=True)
        query, key, value = send(query), send(key), send(value)
    else:
        packed = jnp.concatenate([query, key, value], axis=1)
        packed = lax.all_to_all(packed, "seq", 0, 0, tiled=True)
        query, key, value = packed[:, :HD], packed[:, HD : 2 * HD], packed[:, 2 * HD :]
    result = attend(query, key, value)
    back = lax.all_to_all(result, "seq", 0, 0, tiled=True)
    attended = back.reshape(heads, share, HD, rows // share).transpose(0, 2, 1, 3).reshape(span, rows)
    mine = attended.T.reshape(n_tensor, part, span)
    mine = lax.all_to_all(mine, "tensor", 0, 0, tiled=True)
    mine = mine.transpose(1, 0, 2).reshape(part, n_tensor * span)
    own = lax.dynamic_slice_in_dim(tokens, me * part, part, 0).astype(jnp.float32)
    mixed = own + jnp.dot(mine, w_out_all, preferred_element_type=jnp.float32)
    post = layer_norm(mixed, post_gain).astype(jnp.bfloat16)
    post = lax.all_gather(post, "tensor", axis=0, tiled=True)
    hidden = jax.nn.gelu(
        jnp.dot(post, w_up, preferred_element_type=jnp.float32), approximate=True
    ).astype(jnp.bfloat16)
    term = jnp.dot(hidden, w_down, preferred_element_type=jnp.float32).astype(jnp.bfloat16)
    terms = lax.all_to_all(term.reshape(n_tensor, part, model), "tensor", 0, 0, tiled=True)
    out = (mixed + jnp.sum(terms.astype(jnp.float32), axis=0)).astype(jnp.bfloat16)
    return lax.all_gather(out, "tensor", axis=0, tiled=True)


def solution(mesh):
    placed = (
        P("seq", None),
        P(),
        P(None, None, "tensor"),
        P("tensor", None),
        P(),
        P(None, "tensor"),
        P("tensor", None),
    )
    body = functools.partial(per_device, mesh.shape["seq"], mesh.shape["tensor"])
    return jax.shard_map(
        body, mesh=mesh, in_specs=placed, out_specs=P("seq", None), check_vma=False
    )
```

profile of v0, /device:TPU:0, one launch (start us, length us, event | category | flops | bytes accessed | tf_op | source)
XLA Modules:
  0.0 414.5 jit_solution(9363101909230697513)
XLA Ops:
  6.5 0.0 copy-start
  6.5 0.0 all-gather.6.cloned.1.call-start
  6.5 0.7 all-gather.6.cloned.1.call-update
  7.3 0.0 copy-start.1
  7.3 0.0 copy-start.4
  7.3 0.0 copy-start.5
  7.3 2.1 convert_reduce_fusion
  9.4 0.1 copy-done.1
  9.6 0.7 fusion.2
  10.3 0.0 copy-done.4
  10.3 0.0 copy-done.5
  10.3 2.6 fusion.35
  13.0 0.2 fusion.34
  13.1 0.8 pad_maximum_fusion
  14.0 8.0 %all-to-all-start = ((bf16[16,48,180]{2,1,0:T(8,128)(2,1)}), bf16[16,48,180]{2,1,0:T(8,128)(2,1)S(1)}, u32[]{:S(2)}, u32[]{:S(2)}) async-start(bf16[16,48,180]{2,1,0:T(8,128)(2,1)} %bitcast.3), calls=%async_computation | async-start | bytes 786432 | tf_op jit(solution)/shard_map/all_to_all | solution.py:90
  22.0 1.1 fusion.33
  23.1 51.1 %all-to-all-done.q_ref = bf16[16,48,180]{2,1,0:T(8,128)(2,1)S(1)} async-done(((bf16[16,48,180]{2,1,0:T(8,128)(2,1)}), bf16[16,48,180]{2,1,0:T(8,128)(2,1)S(1)}, u32[]{:S(2)}, u32[]{:S(2)}) %all-to-all-start) | async-done | bytes 276512 | tf_op jit(solution)/shard_map/all_to_all | solution.py:90
  74.1 0.1 broadcast_in_dim.4
  74.2 23.4 %all_to_all.30.k_ref = bf16[16,48,720]{2,1,0:T(8,128)(2,1)} all-to-all(bf16[16,48,720]{2,1,0:T(8,128)(2,1)S(1)} %bitcast.29), channel_id=1, replica_groups=mesh['seq'=16,'tensor'=8] {'seq'}, dimensions={0} | all-to-all | bytes 2211840 | tf_op jit(solution)/shard_map/all_to_all | solution.py:90
  97.6 0.1 broadcast_in_dim.5
  97.7 0.0 copy-done.2
  97.7 22.4 %all_to_all.31.v_ref = bf16[16,48,720]{2,1,0:T(8,128)(2,1)} all-to-all(bf16[16,48,720]{2,1,0:T(8,128)(2,1)S(1)} %bitcast.30), channel_id=1, replica_groups=mesh['seq'=16,'tensor'=8] {'seq'}, dimensions={0} | all-to-all | bytes 2211840 | tf_op jit(solution)/shard_map/all_to_all | solution.py:90
  120.1 130.1 %shard_map.73 = bf16[16,48,180]{2,1,0:T(8,128)(2,1)} custom-call(bf16[16,48,180]{2,1,0:T(8,128)(2,1)} %copy-done.2, bf16[16,48,720]{2,1,0:T(8,128)(2,1)} %all_to_all.30.k_ref, bf16[16,48,720]{2,1,0:T(8,128)(2,1)} %all_to_all.31.v_ref), custom_call_target="tpu_custom_call" | custom-call | flops 50960793600 | bytes 8388608 | tf_op jit(solution)/shard_map/pallas_call | solution.py:49
  250.2 14.2 %all_to_all.32 = bf16[16,48,180]{2,1,0:T(8,128)(2,1)S(1)} all-to-all(bf16[16,48,180]{2,1,0:T(8,128)(2,1)} %shard_map.73), channel_id=1, replica_groups=mesh['seq'=16,'tensor'=8] {'seq'}, dimensions={0} | all-to-all | bytes 552960 | tf_op jit(solution)/shard_map/all_to_all | solution.py:97
  264.4 0.2 copy.15
  264.6 0.3 reshape.71
  264.9 0.4 reshape.72
  265.3 0.8 copy.11
  266.1 3.5 all-to-all-start.4
  269.6 0.2 all-gather.8.cloned.1.call-start
  269.8 8.3 %all-to-all-done.4 = bf16[8,90,192]{1,2,0:T(8,128)(2,1)S(1)} async-done(((bf16[8,90,192]{1,2,0:T(8,128)(2,1)}), bf16[8,90,192]{1,2,0:T(8,128)(2,1)S(1)}, u32[]{:S(2)}, u32[]{:S(2)}) %all-to-all-start.4) | async-done | bytes 276512 | tf_op jit(solution)/shard_map/all_to_all | solution.py:100
  278.1 3.4 fusion.36
  281.5 0.2 multiply_reduce_fusion
  281.8 0.0 copy-done.3
  281.8 0.9 fusion.27
  282.6 0.0 all-gather.8.cloned.1.call-update
  282.6 0.0 all-gather.10.cloned.1.call-start
  282.7 37.5 %all-gather.8.cloned.1.call-done = bf16[8,90,1536]{2,1,0:T(8,128)(2,1)} async-done(((bf16[1,90,1536]{2,1,0:T(8,128)(2,1)}), bf16[8,90,1536]{2,1,0:T(8,128)(2,1)}) %all-gather.8.cloned.1.call-update) | async-done | bytes 2211856 | tf_op jit(solution)/shard_map/all_gather | solution.py:105
  320.2 2.9 reshape.76
  323.1 0.0 copy-done
  323.1 8.2 %convolution_convert_fusion = bf16[720,1536]{1,0:T(8,128)(2,1)} fusion(bf16[768,1536]{1,0:T(8,128)(2,1)S(1)} %copy-done, bf16[720,1536]{1,0:T(8,128)(2,1)} %reshape.76, bf16[1536,768]{1,0:T(8,128)(2,1)} %param.12), kind=kOutput, calls=%fused_computation.9 | convolution fusion | flops 3403468800 | bytes 9142272 | tf_op jit(solution)/shard_map/dot_general | solution.py:109
  331.3 3.0 reshape.74
  334.3 28.9 %all_to_all.33 = bf16[8,90,1536]{2,1,0:T(8,128)(2,1)S(1)} all-to-all(bf16[8,90,1536]{2,1,0:T(8,128)(2,1)} %reshape.74), channel_id=1, replica_groups=mesh['seq'=16,'tensor'=8] {'tensor'}, dimensions={0} | all-to-all | bytes 4423680 | tf_op jit(solution)/shard_map/all_to_all | solution.py:110
  363.1 0.3 convert_reduce_fusion.1
  363.5 0.8 fusion.28
  364.3 0.0 all-gather.10.cloned.1.call-update
  364.3 40.8 %all-gather.10.cloned.1.call-done = bf16[8,90,1536]{2,1,0:T(8,128)(2,1)} async-done(((bf16[1,90,1536]{2,1,0:T(8,128)(2,1)}), bf16[8,90,1536]{2,1,0:T(8,128)(2,1)}) %all-gather.10.cloned.1.call-update) | async-done | bytes 2211856 | tf_op jit(solution)/shard_map/all_gather | solution.py:112
  405.1 2.9 reshape.78
  (8 shorter events, 0.1 us)
Async XLA Ops:
  6.5 316.6 %copy-start = (bf16[768,1536]{1,0:T(8,128)(2,1)S(1)}, bf16[768,1536]{1,0:T(8,128)(2,1)}, u32[]{:S(2)}) copy-start(bf16[768,1536]{1,0:T(8,128)(2,1)} %param.13) | copy-start | bytes 7077892
  6.5 271.5 %all-gather.6.cloned.1.call-start = ((), (), s32[]{:S(2)}) async-start(), calls=%async_computation.6 | async-start | bytes 5308416 | tf_op jit(solution)/shard_map/all_gather | solution.py:76
  7.3 2.3 copy-start.1
  7.3 3.0 copy-start.4
  7.3 3.0 copy-start.5
  14.0 60.2 %all-to-all-start = ((bf16[16,48,180]{2,1,0:T(8,128)(2,1)}), bf16[16,48,180]{2,1,0:T(8,128)(2,1)S(1)}, u32[]{:S(2)}, u32[]{:S(2)}) async-start(bf16[16,48,180]{2,1,0:T(8,128)(2,1)} %bitcast.3), calls=%async_computation | async-start | bytes 786432 | tf_op jit(solution)/shard_map/all_to_all | solution.py:90
  74.1 23.6 %copy-start.2 = (bf16[16,48,180]{2,1,0:T(8,128)(2,1)}, bf16[16,48,180]{2,1,0:T(8,128)(2,1)S(1)}, u32[]{:S(2)}) copy-start(bf16[16,48,180]{2,1,0:T(8,128)(2,1)S(1)} %all-to-all-done.q_ref) | copy-start | bytes 829444
  266.1 12.0 %all-to-all-start.4 = ((bf16[8,90,192]{1,2,0:T(8,128)(2,1)}), bf16[8,90,192]{1,2,0:T(8,128)(2,1)S(1)}, u32[]{:S(2)}, u32[]{:S(2)}) async-start(bf16[8,90,192]{1,2,0:T(8,128)(2,1)} %copy.11), calls=%async_computation.4 | async-start | bytes 786432 | tf_op jit(solution)/shard_map/all_to_all | solution.py:100
  269.6 50.6 %all-gather.8.cloned.1.call-start = ((), (), s32[]{:S(2)}) async-start(), calls=%async_computation.7 | async-start | bytes 2654208 | tf_op jit(solution)/shard_map/all_gather | solution.py:105
  278.1 3.7 copy-start.3
  282.6 122.4 %all-gather.10.cloned.1.call-start = ((), (), s32[]{:S(2)}) async-start(), calls=%async_computation.8 | async-start | bytes 2654208 | tf_op jit(solution)/shard_map/all_gather | solution.py:112
Sparse Core Ops, SparseCore 0:
  9.0 63.2 all-gather.5
  282.8 37.4 all-gather.7
  364.4 40.6 all-gather.9
where the time goes:
time: 415 us
  waiting for transfers between devices  138 us (33%)
  Pallas kernels  130 us (31%)
  blocking collectives  88.8 us (21%)
  matrix products  14.2 us (3%)
  between operations  13.3 us (3%)
  local copies, waits for them, and re-layouts  12.1 us (3%)
  starting transfers between devices  11.7 us (3%)
  other arithmetic  5.96 us (1%)
    pallas_call x1, Pallas kernels, attend(): pl.pallas_call(attend_kernel, grid=(qblocks,), in_specs=[pl.BlockSpec((1,...  130 us
    all_to_all x1, waiting for transfers between devices, per_device(): send = lambda x: lax.all_to_all(x, 'seq', 0, 0, tiled=True)  51.1 us
    all_to_all x2, blocking collectives, per_device(): send = lambda x: lax.all_to_all(x, 'seq', 0, 0, tiled=True)  45.8 us
    all_gather x1, waiting for transfers between devices, per_device(): return lax.all_gather(out, 'tensor', axis=0, tiled=True)  40.8 us
    all_gather x1, waiting for transfers between devices, per_device(): post = lax.all_gather(post, 'tensor', axis=0, tiled=True)  37.5 us
    all_to_all x1, blocking collectives, per_device(): lax.all_to_all(term.reshape(n_tensor, part, model), 'tensor', 0, 0, tiled...  28.9 us
    all_to_all x1, blocking collectives, per_device(): back = lax.all_to_all(result, 'seq', 0, 0, tiled=True)  14.2 us
  transfers between devices with their start and end apart: 5, of which 4 were waited for; matrix products, arithmetic and copies ran while one was open for 2% of the time, Pallas kernels for 31%

commit v1 on v0

v1 whole, which is shorter than its diff:
```python
import functools
import jax
import jax.numpy as jnp
from jax import lax
from jax.experimental import pallas as pl
from jax.experimental.pallas import tpu as pltpu
from jax.sharding import PartitionSpec as P

HD = 48
LOG2E = 1.4426950408889634
MESH = pl.DeviceIdType.MESH
F32 = jnp.float32
BF16 = jnp.bfloat16
RING = 4
BLOCKS = 16
TILES = (slice(0, 256), slice(256, 512), slice(512, 720))


def layer_norm(values, gain):
    mean = jnp.mean(values, axis=-1, keepdims=True)
    centred = values - mean
    var = jnp.mean(centred * centred, axis=-1, keepdims=True)
    return centred * lax.rsqrt(var + 1e-05) * gain


def dot(a, b):
    return jnp.dot(a, b, preferred_element_type=F32)


def remote(src, dst, send, recv, seq):
    return pltpu.make_async_remote_copy(
        src_ref=src, dst_ref=dst, send_sem=send, recv_sem=recv, device_id={"seq": seq}, device_id_type=MESH
    )


def attend_kernel(
    q_ref, kv_ref, out_ref, q_in, kv_in, key_rows, values, acc, peak, scores, obuf,
    q_send, q_recv, y_send, z_send, d_send, kv_recv, o_send, o_recv,
):
    rows = q_ref.shape[2]
    me = lax.axis_index("seq")
    half, y, core = me // (2 * RING), (me // 2) % RING, me % 2

    def at(step):
        return half * (2 * RING) + lax.rem(y + step, RING) * 2 + core

    twin = me - core + (1 - core)
    far = lax.rem(me + 2 * RING, BLOCKS)
    peers = [at(1), at(2), at(3), twin, far]
    barrier = pltpu.get_barrier_semaphore()
    for peer in peers:
        pl.semaphore_signal(barrier, inc=1, device_id={"seq": peer}, device_id_type=MESH)
    pl.semaphore_wait(barrier, len(peers))

    def q_copy(step):
        return remote(
            q_ref.at[lax.rem(y + step, RING)], q_in.at[RING - step], q_send.at[step], q_recv.at[RING - step], at(step)
        )

    def y_copy(step):
        slot = {1: 3, 2: 4, 3: 2}[step]
        return remote(
            kv_ref.at[lax.rem(y + step, RING)], kv_in.at[slot], y_send.at[step], kv_recv.at[slot], at(step)
        )

    def z_copy(src, slot):
        return remote(src, kv_in.at[slot], z_send.at[slot], kv_recv.at[slot], far)

    def d_copy(src, slot):
        return remote(src, kv_in.at[slot], d_send.at[slot], kv_recv.at[slot], twin)

    own = kv_ref.at[y]
    for step in (1, 3, 2):
        q_copy(step).start()
    d_copy(own, 1).start()
    for step in (1, 3, 2):
        y_copy(step).start()
    z_copy(own, 8).start()

    values[:, HD:, :] = jnp.ones((BLOCKS, values.shape[1] - HD, rows), BF16)
    acc[...] = jnp.zeros_like(acc)
    peak[...] = jnp.full_like(peak, -1e30)
    q_in[0] = q_ref[y]
    key_rows[0] = kv_ref[y, :HD].T
    values[0, :HD] = kv_ref[y, HD:]

    def arrive(c):
        d_copy(kv_in.at[c], c).wait_recv()

        @pl.when((c >= 2) & (c <= 4))
        def _():
            d_copy(kv_in.at[c], c + 3).start()
            z_copy(kv_in.at[c], 2 * c + 6).start()

        @pl.when((c >= 8) & (lax.rem(c, 2) == 0))
        def _():
            d_copy(kv_in.at[c], c + 1).start()

        key_rows[c] = kv_in[c, :HD].T
        values[c, :HD] = kv_in[c, HD:]

    def score(c, s, b):
        for lanes in TILES:
            found = dot(key_rows[c], q_in[s, :, lanes])
            scores[b, :rows, lanes] = found
            scores[b, rows : rows + 1, lanes] = jnp.max(found, axis=0, keepdims=True)

    def weigh(c, s, b):
        for lanes in TILES:
            old = peak[s, :, lanes]
            new = jnp.maximum(old, scores[b, rows : rows + 1, lanes])
            peak[s, :, lanes] = new
            weights = jnp.exp2(scores[b, :rows, lanes] - new).astype(BF16)
            acc[s, :, lanes] = acc[s, :, lanes] * jnp.exp2(old - new) + dot(values[c], weights)

    order = (0, 1, 3, 2)

    def block(c, first=False):
        for i, s in enumerate(order):
            b = i % 2
            if i == 2:
                score(c, order[3], 1)
                weigh(c, s, 0)

                @pl.when(c < BLOCKS - 1)
                def _():
                    arrive(c + 1)
            elif i == 3:
                score(jnp.minimum(c + 1, BLOCKS - 1), order[0], 0)
                weigh(c, s, 1)
            else:
                if first:
                    q_copy(RING - order[i + 1]).wait_recv()
                    if i == 1:
                        q_copy(RING - order[3]).wait_recv()
                score(c, order[i + 1], 1 - b)
                weigh(c, s, b)

    score(0, order[0], 0)
    block(jnp.int32(0), True)

    def body(c, carry):
        block(c)
        return carry

    lax.fori_loop(1, BLOCKS, body, 0)

    def o_copy(step):
        return remote(obuf.at[step], out_ref.at[y], o_send.at[step], o_recv.at[RING - step], at(step))

    for s in (2, 1, 3):
        obuf[s] = (acc[s, :HD] / acc[s, HD : HD + 1]).astype(BF16)
        o_copy(s).start()
    out_ref[y] = (acc[0, :HD] / acc[0, HD : HD + 1]).astype(BF16)

    def o_wait(step):
        return remote(
            obuf.at[step], out_ref.at[lax.rem(y + step, RING)], o_send.at[step], o_recv.at[step], at(step)
        )

    for step in (1, 2, 3):
        q_copy(step).wait_send()
        y_copy(step).wait_send()
        o_copy(step).wait_send()
    for slot in (8, 10, 12, 14):
        z_copy(own, slot).wait_send()
    for slot in (1, 5, 6, 7, 9, 11, 13, 15):
        d_copy(own, slot).wait_send()
    for step in (1, 3, 2):
        o_wait(step).wait_recv()


def attend(query, kv):
    heads, width, rows = query.shape
    dma = lambda n: pltpu.SemaphoreType.DMA((n,))
    vmem = pl.BlockSpec(memory_space=pltpu.VMEM)
    return pl.pallas_call(
        attend_kernel,
        in_specs=[vmem, vmem],
        out_specs=vmem,
        out_shape=jax.ShapeDtypeStruct(query.shape, BF16),
        scratch_shapes=[
            pltpu.VMEM((heads, width, rows), BF16),
            pltpu.VMEM((BLOCKS, 2 * width, rows), BF16),
            pltpu.VMEM((BLOCKS, rows, width), BF16),
            pltpu.VMEM((BLOCKS, width + 16, rows), BF16),
            pltpu.VMEM((heads, width + 16, rows), F32),
            pltpu.VMEM((heads, 1, rows), F32),
            pltpu.VMEM((2, rows + 8, rows), F32),
            pltpu.VMEM((heads, width, rows), BF16),
            dma(RING), dma(RING), dma(RING), dma(BLOCKS), dma(BLOCKS), dma(BLOCKS), dma(RING), dma(RING),
        ],
        cost_estimate=pl.CostEstimate(flops=40 * 10**9, bytes_accessed=8 << 20, transcendentals=0),
        compiler_params=pltpu.CompilerParams(
            vmem_limit_bytes=40 << 20, collective_id=0, has_side_effects=True
        ),
    )(query, kv)


def per_device(n_seq, n_tensor, tokens, norm_gain, w_qkv, w_out, post_gain, w_up, w_down):
    rows, model = tokens.shape
    span = w_qkv.shape[2]
    heads = span // HD
    part = rows // n_tensor
    me = lax.axis_index("tensor")

    w_out_all = lax.all_gather(w_out, "tensor", axis=0, tiled=True)

    base = tokens.astype(F32)
    normed = layer_norm(base, norm_gain).astype(BF16)
    qkv = lax.dot_general(
        w_qkv.reshape(model, -1), normed, (((0,), (1,)), ((), ())), preferred_element_type=F32
    ).reshape(3, heads, HD, rows)
    query = (qkv[0] * (LOG2E / HD**0.5)).astype(BF16)
    kv = jnp.concatenate([qkv[1], qkv[2]], axis=1).astype(BF16)
    attended = attend(query, kv).reshape(span, rows)
    mine = attended.T.reshape(n_tensor, part, span)
    mine = lax.all_to_all(mine, "tensor", 0, 0, tiled=True)
    mine = mine.transpose(1, 0, 2).reshape(part, n_tensor * span)
    own = lax.dynamic_slice_in_dim(tokens, me * part, part, 0).astype(F32)
    mixed = own + dot(mine, w_out_all)
    post = layer_norm(mixed, post_gain).astype(BF16)
    post = lax.all_gather(post, "tensor", axis=0, tiled=True)
    hidden = jax.nn.gelu(dot(post, w_up), approximate=True).astype(BF16)
    term = dot(hidden, w_down).astype(BF16)
    terms = lax.all_to_all(term.reshape(n_tensor, part, model), "tensor", 0, 0, tiled=True)
    out = (mixed + jnp.sum(terms.astype(F32), axis=0)).astype(BF16)
    return lax.all_gather(out, "tensor", axis=0, tiled=True)


def solution(mesh):
    placed = (
        P("seq", None),
        P(),
        P(None, None, "tensor"),
        P("tensor", None),
        P(),
        P(None, "tensor"),
        P("tensor", None),
    )
    body = functools.partial(per_device, mesh.shape["seq"], mesh.shape["tensor"])
    return jax.shard_map(
        body, mesh=mesh, in_specs=placed, out_specs=P("seq", None), check_vma=False
    )
```

time: 415 us -> 245 us (0.59)
  blocking collectives: 88.8 us -> 28.8 us
  waiting for transfers between devices: 138 us -> 86.9 us
  Pallas kernels: 130 us -> 83.3 us
  starting transfers between devices: 11.7 us -> 3.72 us
    all_to_all x3 -> x0, blocking collectives: 60 us -> none  [the longest x2 45.8 us: per_device(): send = lambda x: lax.all_to_all(x, 'seq', 0, 0, tiled=True)]
    all_to_all x1 -> x0, waiting for transfers between devices: 51.1 us -> none  [per_device(): send = lambda x: lax.all_to_all(x, 'seq', 0, 0, tiled=True)]
    pallas_call x1, Pallas kernels: 130 us -> 83.3 us  [attend(): pl.pallas_call(attend_kernel, in_specs=[vmem, vmem], out_specs=vmem, out_...]
    all_to_all x1 -> x0, starting transfers between devices: 8 us -> none  [per_device(): send = lambda x: lax.all_to_all(x, 'seq', 0, 0, tiled=True)]
  transfers between devices with their start and end apart: 5 -> 4, of which waited for: 4 -> 3; matrix products, arithmetic and copies ran while one was open for 2% -> 2% of each run, Pallas kernels for 31% -> 34%
where the time goes in v1:
time: 245 us
  waiting for transfers between devices  86.9 us (35%)
  Pallas kernels  83.3 us (34%)
  blocking collectives  28.8 us (12%)
  matrix products  13.3 us (5%)
  between operations  13.2 us (5%)
  local copies, waits for them, and re-layouts  10.2 us (4%)
  other arithmetic  5.19 us (2%)
  starting transfers between devices  3.72 us (2%)
    pallas_call x1, Pallas kernels, attend(): pl.pallas_call(attend_kernel, in_specs=[vmem, vmem], out_specs=vmem, out_...  83.3 us
    all_gather x1, waiting for transfers between devices, per_device(): return lax.all_gather(out, 'tensor', axis=0, tiled=True)  40.8 us
    all_gather x1, waiting for transfers between devices, per_device(): post = lax.all_gather(post, 'tensor', axis=0, tiled=True)  36.6 us
    all_to_all x1, blocking collectives, per_device(): lax.all_to_all(term.reshape(n_tensor, part, model), 'tensor', 0, 0, tiled...  28.8 us
    dot_general x2, matrix products, dot(): return jnp.dot(a, b, preferred_element_type=F32)  11.6 us
    all_to_all x1, waiting for transfers between devices, per_device(): mine = lax.all_to_all(mine, 'tensor', 0, 0, tiled=True)  8.77 us
    unnamed x12, local copies, waits for them, and re-layouts  5.99 us
  transfers between devices with their start and end apart: 4, of which 3 were waited for; matrix products, arithmetic and copies ran while one was open for 2% of the time, Pallas kernels for 34%

profile of v1, /device:TPU:0, one launch (start us, length us, event | category | flops | bytes accessed | tf_op | source)
XLA Modules:
  0.0 244.6 jit_solution(4044223871644730091)
XLA Ops:
  6.5 0.0 copy-start
  6.5 0.0 all-gather.6.cloned.1.call-start
  6.5 0.7 all-gather.6.cloned.1.call-update
  7.3 0.0 copy-start.1
  7.3 0.0 copy-start.3
  7.3 0.0 copy-start.4
  7.3 2.1 convert_reduce_fusion
  9.4 0.1 copy-done.1
  9.6 0.7 fusion.2
  10.3 0.0 copy-done.3
  10.3 0.0 copy-done.4
  10.3 1.7 fusion.34
  12.0 0.1 pad_maximum_fusion.kv_ref
  12.2 83.3 %shard_map.73 = bf16[4,48,720]{2,1,0:T(8,128)(2,1)S(1)} custom-call(bf16[4,48,720]{2,1,0:T(8,128)(2,1)S(1)} %bitcast.24, bf16[4,96,720]{2,1,0:T(8,128)(2,1)S(1)} %pad_maximum_fusion.kv_ref), custom_call_target="tpu_custom_call" | custom-call | flops 40000000000 | bytes 8388608 | tf_op jit(solution)/shard_map/pallas_call | solution.py:177
  95.4 0.4 reshape.53
  95.9 0.8 copy.9
  96.7 3.5 %all-to-all-start = ((bf16[8,90,192]{1,2,0:T(8,128)(2,1)}), bf16[8,90,192]{1,2,0:T(8,128)(2,1)S(1)}, u32[]{:S(2)}, u32[]{:S(2)}) async-start(bf16[8,90,192]{1,2,0:T(8,128)(2,1)} %copy.9), calls=%async_computation | async-start | bytes 786432 | tf_op jit(solution)/shard_map/all_to_all | solution.py:218
  100.1 0.0 all-gather.8.cloned.1.call-start
  100.2 8.8 %all-to-all-done = bf16[8,90,192]{1,2,0:T(8,128)(2,1)S(1)} async-done(((bf16[8,90,192]{1,2,0:T(8,128)(2,1)}), bf16[8,90,192]{1,2,0:T(8,128)(2,1)S(1)}, u32[]{:S(2)}, u32[]{:S(2)}) %all-to-all-start) | async-done | bytes 276512 | tf_op jit(solution)/shard_map/all_to_all | solution.py:218
  108.9 0.0 all-gather.6.cloned.1.call-done
  108.9 0.0 copy-start.2
  109.0 3.4 %fusion.35 = (f32[90]{0:T(128)S(1)}, f32[90,1536]{1,0:T(8,128)S(1)}) fusion(bf16[90,1536]{0,1:T(8,128)(2,1)S(1)} %bitcast.26, bf16[1536,1536]{1,0:T(8,128)(2,1)} %all-gather.6.cloned.1.call-done, bf16[720,1536]{1,0:T(8,128)(2,1)} %param.7, s32[]{:T(128)S(6)} %select_n.3), kind=kOutput, calls=%fused_computation.46 | convolution fusion | flops 425087904 | bytes 5824876 | tf_op jit(solution)/shard_map/dot_general | solution.py:27
  112.4 0.2 multiply_reduce_fusion
  112.6 0.0 copy-done.2
  112.6 0.9 fusion.27
  113.5 0.0 all-gather.8.cloned.1.call-update
  113.5 0.2 all-gather.10.cloned.1.call-start
  113.7 36.6 %all-gather.8.cloned.1.call-done = bf16[8,90,1536]{2,1,0:T(8,128)(2,1)} async-done(((bf16[1,90,1536]{2,1,0:T(8,128)(2,1)}), bf16[8,90,1536]{2,1,0:T(8,128)(2,1)}) %all-gather.8.cloned.1.call-update) | async-done | bytes 2211856 | tf_op jit(solution)/shard_map/all_gather | solution.py:223
  150.3 2.9 %reshape.57 = bf16[720,1536]{1,0:T(8,128)(2,1)} reshape(bf16[8,90,1536]{2,1,0:T(8,128)(2,1)} %all-gather.8.cloned.1.call-done) | data formatting | bytes 4423680
  153.2 0.0 copy-done
  153.2 8.2 %convolution_convert_fusion = bf16[720,1536]{1,0:T(8,128)(2,1)} fusion(bf16[768,1536]{1,0:T(8,128)(2,1)S(1)} %copy-done, bf16[720,1536]{1,0:T(8,128)(2,1)} %reshape.57, bf16[1536,768]{1,0:T(8,128)(2,1)} %param.12), kind=kOutput, calls=%fused_computation.9 | convolution fusion | flops 3403468800 | bytes 9142272 | tf_op jit(solution)/shard_map/dot_general | solution.py:27
  161.4 3.0 %reshape.55 = bf16[8,90,1536]{2,1,0:T(8,128)(2,1)} reshape(bf16[720,1536]{1,0:T(8,128)(2,1)} %convolution_convert_fusion) | data formatting | bytes 4423680 | tf_op jit(solution)/shard_map/reshape | solution.py:226
  164.4 28.8 %all_to_all.10 = bf16[8,90,1536]{2,1,0:T(8,128)(2,1)S(1)} all-to-all(bf16[8,90,1536]{2,1,0:T(8,128)(2,1)} %reshape.55), channel_id=1, replica_groups=mesh['seq'=16,'tensor'=8] {'tensor'}, dimensions={0} | all-to-all | bytes 4423680 | tf_op jit(solution)/shard_map/all_to_all | solution.py:226
  193.2 0.3 convert_reduce_fusion.1
  193.6 0.8 fusion.28
  194.3 0.0 all-gather.10.cloned.1.call-update
  194.4 40.8 %all-gather.10.cloned.1.call-done = bf16[8,90,1536]{2,1,0:T(8,128)(2,1)} async-done(((bf16[1,90,1536]{2,1,0:T(8,128)(2,1)}), bf16[8,90,1536]{2,1,0:T(8,128)(2,1)}) %all-gather.10.cloned.1.call-update) | async-done | bytes 2211856 | tf_op jit(solution)/shard_map/all_gather | solution.py:228
  235.2 2.9 %reshape.59 = bf16[720,1536]{1,0:T(8,128)(2,1)} reshape(bf16[8,90,1536]{2,1,0:T(8,128)(2,1)} %all-gather.10.cloned.1.call-done) | data formatting | bytes 4423680
  (6 shorter events, 0.1 us)
Async XLA Ops:
  6.5 146.7 %copy-start = (bf16[768,1536]{1,0:T(8,128)(2,1)S(1)}, bf16[768,1536]{1,0:T(8,128)(2,1)}, u32[]{:S(2)}) copy-start(bf16[768,1536]{1,0:T(8,128)(2,1)} %param.13) | copy-start | bytes 7077892
  6.5 102.4 %all-gather.6.cloned.1.call-start = ((), (), s32[]{:S(2)}) async-start(), calls=%async_computation.2 | async-start | bytes 5308416 | tf_op jit(solution)/shard_map/all_gather | solution.py:207
  7.3 2.3 copy-start.1
  7.3 3.0 %copy-start.3 = (bf16[1536,3,192]{0,2,1:T(8,128)(2,1)S(1)}, bf16[1536,3,192]{0,2,1:T(8,128)(2,1)}, u32[]{:S(2)}) copy-start(bf16[1536,3,192]{0,2,1:T(8,128)(2,1)} %param.9) | copy-start | bytes 5308420
  7.3 3.0 %copy-start.4 = (f32[1536]{0:T(1024)S(1)}, f32[1536]{0:T(1024)}, u32[]{:S(2)}) copy-start(f32[1536]{0:T(1024)} %param.8) | copy-start | bytes 18436
  96.7 12.3 %all-to-all-start = ((bf16[8,90,192]{1,2,0:T(8,128)(2,1)}), bf16[8,90,192]{1,2,0:T(8,128)(2,1)S(1)}, u32[]{:S(2)}, u32[]{:S(2)}) async-start(bf16[8,90,192]{1,2,0:T(8,128)(2,1)} %copy.9), calls=%async_computation | async-start | bytes 786432 | tf_op jit(solution)/shard_map/all_to_all | solution.py:218
  100.1 50.2 %all-gather.8.cloned.1.call-start = ((), (), s32[]{:S(2)}) async-start(), calls=%async_computation.3 | async-start | bytes 2654208 | tf_op jit(solution)/shard_map/all_gather | solution.py:223
  108.9 3.7 %copy-start.2 = (f32[1536]{0:T(1024)S(1)}, f32[1536]{0:T(1024)}, u32[]{:S(2)}) copy-start(f32[1536]{0:T(1024)} %param.11) | copy-start | bytes 18436
  113.5 121.6 %all-gather.10.cloned.1.call-start = ((), (), s32[]{:S(2)}) async-start(), calls=%async_computation.4 | async-start | bytes 2654208 | tf_op jit(solution)/shard_map/all_gather | solution.py:228
Sparse Core Ops, SparseCore 0:
  9.0 60.0 all-gather.5
  113.6 36.6 all-gather.7
  194.5 40.6 all-gather.9

commit v2 on v1

--- a/solution.py
+++ b/solution.py
@@ -34,8 +34,8 @@
 
 
 def attend_kernel(
-    q_ref, kv_ref, out_ref, q_in, kv_in, key_rows, values, acc, peak, scores, obuf,
-    q_send, q_recv, y_send, z_send, d_send, kv_recv, o_send, o_recv,
+    q_ref, kv_ref, w_ref, out_ref, w_all, q_in, kv_in, key_rows, values, acc, peak, scores, obuf,
+    q_send, q_recv, y_send, z_send, d_send, kv_recv, o_send, o_recv, w_send, w_recv, t_send, t_recv, w_own,
 ):
     rows = q_ref.shape[2]
     me = lax.axis_index("seq")
@@ -47,10 +47,62 @@
     twin = me - core + (1 - core)
     far = lax.rem(me + 2 * RING, BLOCKS)
     peers = [at(1), at(2), at(3), twin, far]
+    tensor = lax.axis_index("tensor")
+    plane, x = tensor // RING, lax.rem(tensor, RING)
+
+    def on(side, step):
+        return side * RING + lax.rem(x + step, RING)
+
+    friends = [on(plane, 1), on(plane, 2), on(plane, 3), on(1 - plane, 0)]
     barrier = pltpu.get_barrier_semaphore()
     for peer in peers:
         pl.semaphore_signal(barrier, inc=1, device_id={"seq": peer}, device_id_type=MESH)
-    pl.semaphore_wait(barrier, len(peers))
+    for friend in friends:
+        pl.semaphore_signal(barrier, inc=1, device_id={"tensor": friend}, device_id_type=MESH)
+    pl.semaphore_wait(barrier, len(peers) + len(friends))
+
+    cut = w_ref.shape[0] // 2
+    rows_of = lambda which: pl.ds(pl.multiple_of(which * cut, cut), cut)
+
+    def w_copy(src, owner, index, friend):
+        return pltpu.make_async_remote_copy(
+            src_ref=src, dst_ref=w_all.at[owner, rows_of(core)], send_sem=w_send.at[index], recv_sem=w_recv.at[index],
+            device_id={"tensor": friend}, device_id_type=MESH,
+        )
+
+    def w_of(side, step, index, friend):
+        owner = on(side, step)
+        return w_copy(w_all.at[owner, rows_of(core)], owner, index, friend)
+
+    def t_copy(index, which):
+        owner = on(plane, index + 1) if index < 3 else on(1 - plane, index - 3)
+        return remote(
+            w_all.at[owner, rows_of(which)], w_all.at[owner, rows_of(which)], t_send.at[index], t_recv.at[index], twin
+        )
+
+    w_mine = w_ref.at[rows_of(core)]
+    w_local = pltpu.make_async_copy(w_ref, w_all.at[tensor], w_own.at[0])
+
+    def arrived(index):
+        w_copy(w_mine, tensor, index, tensor).wait_recv()
+        t_copy(index, core).start()
+
+    def pass_on(c):
+        @pl.when(c == 6)
+        def _():
+            arrived(3)
+            for step in (1, 3, 2):
+                w_copy(w_all.at[on(1 - plane, 0), rows_of(core)], on(1 - plane, 0), 3 + RING - step, on(plane, step)).start()
+
+        @pl.when(c == 10)
+        def _():
+            for index in (0, 2, 1):
+                arrived(index)
+
+        @pl.when(c == BLOCKS - 1)
+        def _():
+            for index in (4, 6, 5):
+                arrived(index)
 
     def q_copy(step):
         return remote(
@@ -76,11 +128,16 @@
     for step in (1, 3, 2):
         y_copy(step).start()
     z_copy(own, 8).start()
+    w_local.start()
+    w_copy(w_mine, tensor, 3, on(1 - plane, 0)).start()
+    for step in (1, 3, 2):
+        w_copy(w_mine, tensor, RING - step - 1, on(plane, step)).start()
 
     values[:, HD:, :] = jnp.ones((BLOCKS, values.shape[1] - HD, rows), BF16)
     acc[...] = jnp.zeros_like(acc)
     peak[...] = jnp.full_like(peak, -1e30)
     q_in[0] = q_ref[y]
+    obuf[:, :, rows:] = jnp.zeros((RING, HD, obuf.shape[2] - rows), BF16)
     key_rows[0] = kv_ref[y, :HD].T
     values[0, :HD] = kv_ref[y, HD:]
 
@@ -96,8 +153,7 @@
         def _():
             d_copy(kv_in.at[c], c + 1).start()
 
-        key_rows[c] = kv_in[c, :HD].T
-        values[c, :HD] = kv_in[c, HD:]
+        pass_on(c)
 
     def score(c, s, b):
         for lanes in TILES:
@@ -116,25 +172,24 @@
     order = (0, 1, 3, 2)
 
     def block(c, first=False):
+        after = jnp.minimum(c + 1, BLOCKS - 1)
+        if first:
+            arrive(after)
+        else:
+            @pl.when(c < BLOCKS - 1)
+            def _():
+                arrive(after)
+
+        key_rows[after] = kv_in[after, :HD].T
+        values[after, :HD] = kv_in[after, HD:]
         for i, s in enumerate(order):
-            b = i % 2
-            if i == 2:
-                score(c, order[3], 1)
-                weigh(c, s, 0)
-
-                @pl.when(c < BLOCKS - 1)
-                def _():
-                    arrive(c + 1)
-            elif i == 3:
-                score(jnp.minimum(c + 1, BLOCKS - 1), order[0], 0)
-                weigh(c, s, 1)
+            if first and i < 3:
+                q_copy(RING - order[i + 1]).wait_recv()
+            if i < 3:
+                score(c, order[i + 1], 1 - i % 2)
             else:
-                if first:
-                    q_copy(RING - order[i + 1]).wait_recv()
-                    if i == 1:
-                        q_copy(RING - order[3]).wait_recv()
-                score(c, order[i + 1], 1 - b)
-                weigh(c, s, b)
+                score(after, order[0], 0)
+            weigh(c, s, i % 2)
 
     score(0, order[0], 0)
     block(jnp.int32(0), True)
@@ -149,9 +204,10 @@
         return remote(obuf.at[step], out_ref.at[y], o_send.at[step], o_recv.at[RING - step], at(step))
 
     for s in (2, 1, 3):
-        obuf[s] = (acc[s, :HD] / acc[s, HD : HD + 1]).astype(BF16)
+        obuf[s, :, :rows] = (acc[s, :HD] / acc[s, HD : HD + 1]).astype(BF16)
         o_copy(s).start()
-    out_ref[y] = (acc[0, :HD] / acc[0, HD : HD + 1]).astype(BF16)
+    out_ref[y, :, :rows] = (acc[0, :HD] / acc[0, HD : HD + 1]).astype(BF16)
+    out_ref[y, :, rows:] = jnp.zeros((HD, out_ref.shape[2] - rows), BF16)
 
     def o_wait(step):
         return remote(
@@ -166,19 +222,27 @@
         z_copy(own, slot).wait_send()
     for slot in (1, 5, 6, 7, 9, 11, 13, 15):
         d_copy(own, slot).wait_send()
+    for index in range(7):
+        w_copy(w_mine, tensor, index, tensor).wait_send()
+        t_copy(index, core).wait_send()
+        t_copy(index, 1 - core).wait_recv()
+    w_local.wait()
     for step in (1, 3, 2):
         o_wait(step).wait_recv()
 
 
-def attend(query, kv):
+def attend(query, kv, w_out, padded, n_tensor):
     heads, width, rows = query.shape
     dma = lambda n: pltpu.SemaphoreType.DMA((n,))
     vmem = pl.BlockSpec(memory_space=pltpu.VMEM)
     return pl.pallas_call(
         attend_kernel,
-        in_specs=[vmem, vmem],
-        out_specs=vmem,
-        out_shape=jax.ShapeDtypeStruct(query.shape, BF16),
+        in_specs=[vmem, vmem, vmem],
+        out_specs=[vmem, pl.BlockSpec(memory_space=pl.ANY)],
+        out_shape=[
+            jax.ShapeDtypeStruct((heads, width, padded), BF16),
+            jax.ShapeDtypeStruct((n_tensor, *w_out.shape), BF16),
+        ],
         scratch_shapes=[
             pltpu.VMEM((heads, width, rows), BF16),
             pltpu.VMEM((BLOCKS, 2 * width, rows), BF16),
@@ -187,24 +251,181 @@
             pltpu.VMEM((heads, width + 16, rows), F32),
             pltpu.VMEM((heads, 1, rows), F32),
             pltpu.VMEM((2, rows + 8, rows), F32),
-            pltpu.VMEM((heads, width, rows), BF16),
+            pltpu.VMEM((heads, width, padded), BF16),
             dma(RING), dma(RING), dma(RING), dma(BLOCKS), dma(BLOCKS), dma(BLOCKS), dma(RING), dma(RING),
+            dma(7), dma(7), dma(7), dma(7), dma(1),
         ],
         cost_estimate=pl.CostEstimate(flops=40 * 10**9, bytes_accessed=8 << 20, transcendentals=0),
         compiler_params=pltpu.CompilerParams(
             vmem_limit_bytes=40 << 20, collective_id=0, has_side_effects=True
         ),
-    )(query, kv)
+    )(query, kv, w_out)
+
+
+class Tensor:
+    def __init__(self):
+        self.me = lax.axis_index("tensor")
+        self.plane, self.x = self.me // RING, lax.rem(self.me, RING)
+        self.right, self.left = self.on(self.plane, 1), self.on(self.plane, 3)
+        self.pair = self.on(1 - self.plane, 0)
+
+    def on(self, side, step):
+        return side * RING + lax.rem(self.x + step, RING)
+
+    def meet(self):
+        barrier = pltpu.get_barrier_semaphore()
+        for friend in (self.right, self.left, self.pair):
+            pl.semaphore_signal(barrier, inc=1, device_id={"tensor": friend}, device_id_type=MESH)
+        pl.semaphore_wait(barrier, 3)
+
+
+def send(src, dst, send_sem, recv_sem, friend):
+    return pltpu.make_async_remote_copy(
+        src_ref=src, dst_ref=dst, send_sem=send_sem, recv_sem=recv_sem,
+        device_id={"tensor": friend}, device_id_type=MESH,
+    )
+
+
+def gather(t, mine, buf, cut, send_sem, recv_sem):
+    lo, hi = pl.ds(0, cut), pl.ds(cut, cut)
+    copies = {
+        "right": (mine, t.me, None, t.right, 0),
+        "left": (mine, t.me, None, t.left, 1),
+        "pair": (mine, t.me, None, t.pair, 2),
+        "far lo": (None, t.left, lo, t.right, 3),
+        "far hi": (None, t.right, hi, t.left, 4),
+        "over right": (None, t.pair, None, t.right, 5),
+        "over left": (None, t.pair, None, t.left, 6),
+        "pair lo": (None, t.on(t.plane, 2), lo, t.pair, 7),
+        "pair hi": (None, t.on(t.plane, 2), hi, t.pair, 8),
+    }
+
+    def copy(name):
+        src, block, part, to, i = copies[name]
+        dst = buf.at[block] if part is None else buf.at[block, part]
+        return send(dst if src is None else src, dst, send_sem.at[i], recv_sem.at[i], to)
+
+    for name in ("right", "left", "pair"):
+        copy(name).start()
+    copy("right").wait_recv()
+    copy("far lo").start()
+    copy("left").wait_recv()
+    copy("far hi").start()
+    copy("pair").wait_recv()
+    copy("over right").start()
+    copy("over left").start()
+    copy("far lo").wait_recv()
+    copy("pair lo").start()
+    copy("far hi").wait_recv()
+    copy("pair hi").start()
+    for name in ("over right", "over left", "pair lo", "pair hi"):
+        copy(name).wait_recv()
+    for name in copies:
+        copy(name).wait_send()
+
+
+def gather_kernel(x_ref, out_ref, send_sem, recv_sem):
+    t = Tensor()
+    t.meet()
+    out_ref[t.me] = x_ref[...]
+    gather(t, x_ref, out_ref, x_ref.shape[0] // 2, send_sem, recv_sem)
+
+
+def gather_heads(x, n_tensor):
+    dma = lambda n: pltpu.SemaphoreType.DMA((n,))
+    return pl.pallas_call(
+        gather_kernel,
+        in_specs=[pl.BlockSpec(memory_space=pltpu.VMEM)],
+        out_specs=pl.BlockSpec(memory_space=pltpu.VMEM),
+        out_shape=jax.ShapeDtypeStruct((n_tensor, *x.shape), x.dtype),
+        scratch_shapes=[dma(9), dma(9)],
+        cost_estimate=pl.CostEstimate(flops=20 * 10**9, bytes_accessed=8 << 20, transcendentals=0),
+        compiler_params=pltpu.CompilerParams(vmem_limit_bytes=16 << 20, collective_id=1, has_side_effects=True),
+    )(x)
+
+
+def finish_kernel(
+    term_ref, mixed_ref, out_ref, own, far_in, over_in, half_in, edge_in, pair_in, far_sum, over_sum, edge_sum,
+    s_send, s_recv, g_send, g_recv,
+):
+    t = Tensor()
+    part = mixed_ref.shape[0]
+    cut = part // 2
+    lo, hi = pl.ds(0, cut), pl.ds(cut, cut)
+    there = 1 - t.plane
+    t.meet()
+    copies = {}
+
+    def go(name, src, dst, to):
+        i = len(copies)
+        copies[name] = send(src, dst, s_send.at[i], s_recv.at[i], to)
+        copies[name].start()
+
+    wait = lambda name: copies[name].wait_recv()
+    far, far_over = t.on(t.plane, 2), t.on(there, 2)
+    go("far", term_ref.at[far_over], far_in, t.pair)
+    go("over right", term_ref.at[t.on(there, 1)], over_in.at[0], t.right)
+    go("over left", term_ref.at[t.on(there, 3)], over_in.at[1], t.left)
+    go("edge right", term_ref.at[t.right, lo], edge_in.at[0, lo], t.right)
+    go("edge left", term_ref.at[t.left, hi], edge_in.at[1, hi], t.left)
+    wait("far")
+    far_sum[...] = (far_in[...].astype(F32) + term_ref[far].astype(F32)).astype(BF16)
+    go("half left", far_sum.at[lo], half_in.at[0], t.left)
+    go("half right", far_sum.at[hi], half_in.at[1], t.right)
+    wait("over right")
+    wait("over left")
+    over_sum[...] = (
+        over_in[0].astype(F32) + over_in[1].astype(F32) + term_ref[t.pair].astype(F32)
+    ).astype(BF16)
+    go("pair", over_sum, pair_in, t.pair)
+    wait("half left")
+    edge_sum[0] = (half_in[0].astype(F32) + term_ref[t.left, lo].astype(F32)).astype(BF16)
+    go("sum left", edge_sum.at[0], edge_in.at[1, lo], t.left)
+    wait("half right")
+    edge_sum[1] = (half_in[1].astype(F32) + term_ref[t.right, hi].astype(F32)).astype(BF16)
+    go("sum right", edge_sum.at[1], edge_in.at[0, hi], t.right)
+    for name in ("edge right", "edge left", "sum left", "sum right", "pair"):
+        wait(name)
+    own[...] = (
+        mixed_ref[...]
+        + term_ref[t.me].astype(F32)
+        + edge_in[0].astype(F32)
+        + edge_in[1].astype(F32)
+        + pair_in[...].astype(F32)
+    ).astype(BF16)
+    out_ref[t.me] = own[...]
+    for name in copies:
+        copies[name].wait_send()
+    gather(t, own, out_ref, cut, g_send, g_recv)
+
+
+def finish(term, mixed):
+    n_tensor, part, model = term.shape
+    dma = lambda n: pltpu.SemaphoreType.DMA((n,))
+    vmem = pl.BlockSpec(memory_space=pltpu.VMEM)
+    block = lambda *lead: pltpu.VMEM((*lead, part, model), BF16)
+    half = pltpu.VMEM((2, part // 2, model), BF16)
+    return pl.pallas_call(
+        finish_kernel,
+        in_specs=[vmem, vmem],
+        out_specs=vmem,
+        out_shape=jax.ShapeDtypeStruct(term.shape, BF16),
+        scratch_shapes=[
+            block(), block(), block(2), half, block(2), block(), block(), block(), half,
+            dma(10), dma(10), dma(9), dma(9),
+        ],
+        cost_estimate=pl.CostEstimate(flops=40 * 10**9, bytes_accessed=8 << 20, transcendentals=0),
+        compiler_params=pltpu.CompilerParams(vmem_limit_bytes=32 << 20, collective_id=2, has_side_effects=True),
+    )(term, mixed)
 
 
 def per_device(n_seq, n_tensor, tokens, norm_gain, w_qkv, w_out, post_gain, w_up, w_down):
     rows, model = tokens.shape
     span = w_qkv.shape[2]
     heads = span // HD
-    part = rows // n_tensor
+    part = -(-rows // (16 * n_tensor)) * 16
+    padded = n_tensor * part
     me = lax.axis_index("tensor")
-
-    w_out_all = lax.all_gather(w_out, "tensor", axis=0, tiled=True)
 
     base = tokens.astype(F32)
     normed = layer_norm(base, norm_gain).astype(BF16)
@@ -213,19 +434,16 @@
     ).reshape(3, heads, HD, rows)
     query = (qkv[0] * (LOG2E / HD**0.5)).astype(BF16)
     kv = jnp.concatenate([qkv[1], qkv[2]], axis=1).astype(BF16)
-    attended = attend(query, kv).reshape(span, rows)
-    mine = attended.T.reshape(n_tensor, part, span)
-    mine = lax.all_to_all(mine, "tensor", 0, 0, tiled=True)
-    mine = mine.transpose(1, 0, 2).reshape(part, n_tensor * span)
-    own = lax.dynamic_slice_in_dim(tokens, me * part, part, 0).astype(F32)
-    mixed = own + dot(mine, w_out_all)
+    attended, w_out_all = attend(query, kv, w_out, padded, n_tensor)
+    attended = gather_heads(attended.reshape(span, padded), n_tensor).reshape(n_tensor * span, padded)
+    mixed = jnp.pad(base, ((0, padded - rows), (0, 0))) + lax.dot_general(
+        attended, w_out_all.reshape(n_tensor * span, model), (((0,), (0,)), ((), ())), preferred_element_type=F32
+    )
     post = layer_norm(mixed, post_gain).astype(BF16)
-    post = lax.all_gather(post, "tensor", axis=0, tiled=True)
     hidden = jax.nn.gelu(dot(post, w_up), approximate=True).astype(BF16)
-    term = dot(hidden, w_down).astype(BF16)
-    terms = lax.all_to_all(term.reshape(n_tensor, part, model), "tensor", 0, 0, tiled=True)
-    out = (mixed + jnp.sum(terms.astype(F32), axis=0)).astype(BF16)
-    return lax.all_gather(out, "tensor", axis=0, tiled=True)
+    term = dot(hidden, w_down).astype(BF16).reshape(n_tensor, part, model)
+    own = lax.dynamic_slice_in_dim(mixed, me * part, part, 0)
+    return finish(term, own).reshape(padded, model)[:rows]
 
 
 def solution(mesh):

time: 245 us -> 140 us (0.57)
  waiting for transfers between devices: 86.9 us -> 0 us
  Pallas kernels: 83.3 us -> 113 us
  blocking collectives: 28.8 us -> 0 us
  between operations: 13.2 us -> 0.15 us
  starting transfers between devices: 3.72 us -> 0 us
  local copies, waits for them, and re-layouts: 10.2 us -> 6.99 us
    all_gather x3 -> x0, waiting for transfers between devices: 77.4 us -> none  [the longest x1 40.8 us: per_device(): return lax.all_gather(out, 'tensor', axis=0, tiled=True)]
    pallas_call x1 -> x3, Pallas kernels: 83.3 us -> 113 us  [the longest x1 53.3 us: attend(): pl.pallas_call(attend_kernel, in_specs=[vmem, vmem, vmem], out_specs=[vme...]
    all_to_all x1 -> x0, blocking collectives: 28.8 us -> none  [per_device(): lax.all_to_all(term.reshape(n_tensor, part, model), 'tensor', 0, 0, tiled...]
    all_to_all x1 -> x0, waiting for transfers between devices: 8.77 us -> none  [per_device(): mine = lax.all_to_all(mine, 'tensor', 0, 0, tiled=True)]
    reshape x3 -> x0, local copies, waits for them, and re-layouts: 4.21 us -> none  [the longest x1 2.96 us: per_device(): term.reshape(n_tensor, part, model)]
    dot_general x0 -> x1, matrix products: none -> 4.12 us  [per_device(): lax.dot_general(attended, w_out_all.reshape(n_tensor * span, model), (((0...]
    all_to_all x1 -> x0, starting transfers between devices: 3.45 us -> none  [per_device(): mine = lax.all_to_all(mine, 'tensor', 0, 0, tiled=True)]
    dot_general x2 -> x1, matrix products: 11.6 us -> 9.34 us  [dot(): return jnp.dot(a, b, preferred_element_type=F32)]
  transfers between devices with their start and end apart: 4 -> 0, of which waited for: 3 -> 0; matrix products, arithmetic and copies ran while one was open for 2% -> 0% of each run, Pallas kernels for 34% -> 0%
where the time goes in v2:
time: 140 us
  Pallas kernels  113 us (81%)
  matrix products  15.1 us (11%)
  local copies, waits for them, and re-layouts  6.99 us (5%)
  other arithmetic  4.14 us (3%)
    pallas_call x1, Pallas kernels, attend(): pl.pallas_call(attend_kernel, in_specs=[vmem, vmem, vmem], out_specs=[vme...  53.3 us
    pallas_call x1, Pallas kernels, finish(): pl.pallas_call(finish_kernel, in_specs=[vmem, vmem], out_specs=vmem, out_...  38.6 us
    pallas_call x1, Pallas kernels, gather_heads(): pl.pallas_call(gather_kernel, in_specs=[pl.BlockSpec(memory_space=pltpu.V...  21.3 us
    dot_general x1, matrix products, dot(): return jnp.dot(a, b, preferred_element_type=F32)  9.34 us
    unnamed x16, local copies, waits for them, and re-layouts  4.35 us
    dot_general x1, matrix products, per_device(): lax.dot_general(attended, w_out_all.reshape(n_tensor * span, model), (((0...  4.12 us

profile of v2, /device:TPU:0, one launch (start us, length us, event | category | flops | bytes accessed | tf_op | source)
XLA Modules:
  0.0 139.6 jit_solution(2230953647455166815)
XLA Ops:
  0.0 0.0 copy-start
  0.0 0.0 copy-start.4
  0.0 0.0 copy-start.5
  0.0 0.0 copy-start.6
  0.0 2.1 %convert_reduce_fusion = f32[720]{0:T(1024)S(1)} fusion(bf16[720,1536]{1,0:T(8,128)(2,1)} %param.7), kind=kLoop, calls=%fused_computation.7 | loop fusion | flops 2211120 | bytes 2214720 | tf_op jit(solution)/shard_map/reduce_sum | solution.py:20
  2.2 0.3 copy-done.4
  2.4 0.7 multiply_reduce_fusion.1
  3.2 0.0 copy-done.5
  3.2 0.0 copy-done.6
  3.2 1.7 %fusion.23 = (bf16[576,720]{1,0:T(8,128)(2,1)S(1)}, f32[576,720]{1,0:T(8,128)S(1)}) fusion(bf16[1536,576]{0,1:T(8,128)(2,1)S(1)} %bitcast.22, bf16[720,1536]{1,0:T(8,128)(2,1)S(1)} %copy-done.4, f32[1536]{0:T(1024)S(1)} %copy-done.6, f32[720]{0:T(1024)S(1)} %add_rsqrt_fusion.1, f32[720]{0:T(1024)S(1)} %broadcast_multiply_fusion.1), kind=kOutput, calls=%fused_computation.38 | convolution fusion | flops 1279964160 | bytes 6481536 | tf_op jit(solution)/shard_map/dot_general | solution.py:432
  4.9 0.0 copy-start.1
  4.9 0.1 pad_maximum_fusion.kv_ref
  5.0 0.9 copy-done.1
  5.9 53.3 %shard_map.73 = (bf16[4,48,768]{2,1,0:T(8,128)(2,1)S(1)}, bf16[8,192,1536]{2,1,0:T(8,128)(2,1)S(1)}) custom-call(bf16[4,48,720]{2,1,0:T(8,128)(2,1)S(1)} %bitcast.17, bf16[4,96,720]{2,1,0:T(8,128)(2,1)S(1)} %pad_maximum_fusion.kv_ref, bf16[192,1536]{1,0:T(8,128)(2,1)S(1)} %copy-done.1), custom_call_target="tpu_custom_call" | custom-call | flops 40000000000 | bytes 8388608 | tf_op jit(solution)/shard_map/pallas_call | solution.py:238
  59.2 21.3 %shard_map.74 = bf16[8,192,768]{2,1,0:T(8,128)(2,1)S(1)} custom-call(bf16[192,768]{1,0:T(8,128)(2,1)S(1)} %bitcast.19), custom_call_target="tpu_custom_call" | custom-call | flops 20000000000 | bytes 8388608 | tf_op jit(solution)/shard_map/pallas_call | solution.py:336
  80.5 0.6 convert_element_type.23
  81.1 4.1 %fusion.24 = (f32[768]{0:T(1024)S(1)}, f32[768,1536]{1,0:T(8,128)S(1)}) fusion(bf16[8,192,768]{2,1,0:T(8,128)(2,1)S(1)} %shard_map.74, bf16[8,192,1536]{2,1,0:T(8,128)(2,1)S(1)} %get-tuple-element.8, f32[720,1536]{1,0:T(8,128)S(1)} %convert_element_type.23), kind=kOutput, calls=%fused_computation.39 | convolution fusion | flops 3626237184 | bytes 16223232 | tf_op jit(solution)/shard_map/dot_general | solution.py:439
  85.2 0.0 copy-start.3
  85.2 0.0 copy-start.7
  85.2 0.6 multiply_reduce_fusion
  85.8 1.5 %copy-done.3 = f32[768,1536]{1,0:T(8,128)} copy-done((f32[768,1536]{1,0:T(8,128)}, f32[768,1536]{1,0:T(8,128)S(1)}, u32[]{:S(2)}) %copy-start.3) | copy-done | bytes 4718616
  87.3 0.0 copy-done
  87.3 0.0 copy-done.7
  87.3 9.3 %convolution_convert_fusion = bf16[768,1536]{1,0:T(8,128)(2,1)} fusion(bf16[768,1536]{1,0:T(8,128)(2,1)S(1)} %copy-done, bf16[1536,768]{1,0:T(8,128)(2,1)} %param.12, f32[768,1536]{1,0:T(8,128)} %copy-done.3, f32[1536]{0:T(1024)S(1)} %copy-done.7, f32[768]{0:T(1024)S(1)} %add_rsqrt_fusion, f32[768]{0:T(1024)S(1)} %broadcast_multiply_fusion), kind=kOutput, calls=%fused_computation.6 | convolution fusion | flops 3635085312 | bytes 11808768 | tf_op jit(solution)/shard_map/dot_general | solution.py:27
  96.7 1.1 constant_dynamic-slice_fusion.mixed_ref
  97.8 0.0 copy-start.2
  97.8 1.7 %copy-done.2 = bf16[768,1536]{1,0:T(8,128)(2,1)S(1)} copy-done((bf16[768,1536]{1,0:T(8,128)(2,1)S(1)}, bf16[768,1536]{1,0:T(8,128)(2,1)}, u32[]{:S(2)}) %copy-start.2) | copy-done | bytes 2359320
  99.4 38.6 %shard_map.75 = bf16[8,96,1536]{2,1,0:T(8,128)(2,1)S(1)} custom-call(bf16[8,96,1536]{2,1,0:T(8,128)(2,1)S(1)} %bitcast.18, f32[96,1536]{1,0:T(8,128)S(1)} %constant_dynamic-slice_fusion.mixed_ref), custom_call_target="tpu_custom_call" | custom-call | flops 40000000000 | bytes 8388608 | tf_op jit(solution)/shard_map/pallas_call | solution.py:408
  138.1 1.5 %slice.24 = bf16[720,1536]{1,0:T(8,128)(2,1)} slice(bf16[768,1536]{1,0:T(8,128)(2,1)S(1)} %bitcast.16), slice={[0:720], [0:1536]} | slice | bytes 4423680 | tf_op jit(solution)/shard_map/slice | solution.py:446
  (6 shorter events, 0.1 us)
Async XLA Ops:
  0.0 87.3 %copy-start = (bf16[768,1536]{1,0:T(8,128)(2,1)S(1)}, bf16[768,1536]{1,0:T(8,128)(2,1)}, u32[]{:S(2)}) copy-start(bf16[768,1536]{1,0:T(8,128)(2,1)} %param.13) | copy-start | bytes 7077892
  0.0 2.4 %copy-start.4 = (bf16[720,1536]{1,0:T(8,128)(2,1)S(1)}, bf16[720,1536]{1,0:T(8,128)(2,1)}, u32[]{:S(2)}) copy-start(bf16[720,1536]{1,0:T(8,128)(2,1)} %param.7) | copy-start | bytes 6635524
  0.0 3.2 %copy-start.5 = (bf16[1536,3,192]{0,2,1:T(8,128)(2,1)S(1)}, bf16[1536,3,192]{0,2,1:T(8,128)(2,1)}, u32[]{:S(2)}) copy-start(bf16[1536,3,192]{0,2,1:T(8,128)(2,1)} %param.9) | copy-start | bytes 5308420
  0.0 3.2 %copy-start.6 = (f32[1536]{0:T(1024)S(1)}, f32[1536]{0:T(1024)}, u32[]{:S(2)}) copy-start(f32[1536]{0:T(1024)} %param.8) | copy-start | bytes 18436
  4.9 1.1 copy-start.1
  85.2 2.1 %copy-start.3 = (f32[768,1536]{1,0:T(8,128)}, f32[768,1536]{1,0:T(8,128)S(1)}, u32[]{:S(2)}) copy-start(f32[768,1536]{1,0:T(8,128)S(1)} %get-tuple-element.14) | copy-start | bytes 14155780
  85.2 2.1 %copy-start.7 = (f32[1536]{0:T(1024)S(1)}, f32[1536]{0:T(1024)}, u32[]{:S(2)}) copy-start(f32[1536]{0:T(1024)} %param.11) | copy-start | bytes 18436
  97.8 1.7 %copy-start.2 = (bf16[768,1536]{1,0:T(8,128)(2,1)S(1)}, bf16[768,1536]{1,0:T(8,128)(2,1)}, u32[]{:S(2)}) copy-start(bf16[768,1536]{1,0:T(8,128)(2,1)} %convolution_convert_fusion) | copy-start | bytes 7077892

commit v3 on v2

--- a/solution.py
+++ b/solution.py
@@ -34,8 +34,9 @@
 
 
 def attend_kernel(
-    q_ref, kv_ref, w_ref, out_ref, w_all, q_in, kv_in, key_rows, values, acc, peak, scores, obuf,
+    q_ref, kv_ref, w_hbm, up_ref, down_ref, out_ref, w_all, up_all, down_all, w_ref, q_in, kv_in, key_rows, values, acc, peak, scores, obuf,
     q_send, q_recv, y_send, z_send, d_send, kv_recv, o_send, o_recv, w_send, w_recv, t_send, t_recv, w_own,
+    f_send, f_recv, g_send, g_recv, h_send, h_recv,
 ):
     rows = q_ref.shape[2]
     me = lax.axis_index("seq")
@@ -59,7 +60,48 @@
         pl.semaphore_signal(barrier, inc=1, device_id={"seq": peer}, device_id_type=MESH)
     for friend in friends:
         pl.semaphore_signal(barrier, inc=1, device_id={"tensor": friend}, device_id_type=MESH)
-    pl.semaphore_wait(barrier, len(peers) + len(friends))
+    across = on(1 - plane, 0)
+    pl.semaphore_signal(barrier, inc=1, device_id={"seq": far, "tensor": across}, device_id_type=MESH)
+    w_load = pltpu.make_async_copy(w_hbm, w_ref, w_own.at[0])
+    w_load.start()
+    values[:, HD:, :] = jnp.ones((BLOCKS, values.shape[1] - HD, rows), BF16)
+    acc[...] = jnp.zeros_like(acc)
+    peak[...] = jnp.full_like(peak, -1e30)
+    q_in[0] = q_ref[y]
+    obuf[:, :, rows:] = jnp.zeros((RING, HD, obuf.shape[2] - rows), BF16)
+    key_rows[0] = kv_ref[y, :HD].T
+    values[0, :HD] = kv_ref[y, HD:]
+    pl.semaphore_wait(barrier, len(peers) + len(friends) + 1)
+
+    pieces = 2 * RING
+    both = ((up_ref, up_all), (down_ref, down_all))
+
+    def piece(j, which):
+        return lax.rem(y + (0, 2, 1, 3)[j], RING) * 2 + which
+
+    def f_copy(k, j):
+        ref, whole = both[k]
+        size = ref.shape[0] // pieces
+        number = piece(j, core)
+        src = ref.at[pl.ds(pl.multiple_of(number * size, size), size)]
+        device = {"tensor": across} if k == 0 else {"seq": far, "tensor": across}
+        return pltpu.make_async_remote_copy(
+            src_ref=src, dst_ref=whole.at[number], send_sem=f_send.at[2 * k + j], recv_sem=f_recv.at[2 * k + j],
+            device_id=device, device_id_type=MESH,
+        )
+
+    def g_copy(k, step):
+        whole = both[k][1]
+        number = piece(0, core)
+        i = 2 * k + step // 2
+        j = 2 * k + 1 - step // 2
+        return remote(whole.at[number], whole.at[number], g_send.at[i], g_recv.at[j], at(step))
+
+    def h_copy(k, j, which):
+        whole = both[k][1]
+        number = piece(j, which)
+        i = 4 * k + j
+        return remote(whole.at[number], whole.at[number], h_send.at[i], h_recv.at[i], twin)
 
     cut = w_ref.shape[0] // 2
     rows_of = lambda which: pl.ds(pl.multiple_of(which * cut, cut), cut)
@@ -81,13 +123,36 @@
         )
 
     w_mine = w_ref.at[rows_of(core)]
-    w_local = pltpu.make_async_copy(w_ref, w_all.at[tensor], w_own.at[0])
+    w_local = pltpu.make_async_copy(w_ref, w_all.at[tensor], w_own.at[1])
 
     def arrived(index):
         w_copy(w_mine, tensor, index, tensor).wait_recv()
         t_copy(index, core).start()
 
     def pass_on(c):
+        @pl.when(c == 5)
+        def _():
+            for k in range(2):
+                f_copy(k, 1).start()
+                f_copy(k, 0).wait_recv()
+                for step in (1, 3):
+                    g_copy(k, step).start()
+                h_copy(k, 0, core).start()
+
+        @pl.when(c == 13)
+        def _():
+            for k in range(2):
+                for step in (1, 3):
+                    g_copy(k, step).wait_recv()
+                for j in (2, 3):
+                    h_copy(k, j, core).start()
+
+        @pl.when(c == BLOCKS - 1)
+        def _():
+            for k in range(2):
+                f_copy(k, 1).wait_recv()
+                h_copy(k, 1, core).start()
+
         @pl.when(c == 6)
         def _():
             arrived(3)
@@ -128,18 +193,13 @@
     for step in (1, 3, 2):
         y_copy(step).start()
     z_copy(own, 8).start()
+    f_copy(0, 0).start()
+    f_copy(1, 0).start()
+    w_load.wait()
     w_local.start()
-    w_copy(w_mine, tensor, 3, on(1 - plane, 0)).start()
+    w_copy(w_mine, tensor, 3, across).start()
     for step in (1, 3, 2):
         w_copy(w_mine, tensor, RING - step - 1, on(plane, step)).start()
-
-    values[:, HD:, :] = jnp.ones((BLOCKS, values.shape[1] - HD, rows), BF16)
-    acc[...] = jnp.zeros_like(acc)
-    peak[...] = jnp.full_like(peak, -1e30)
-    q_in[0] = q_ref[y]
-    obuf[:, :, rows:] = jnp.zeros((RING, HD, obuf.shape[2] - rows), BF16)
-    key_rows[0] = kv_ref[y, :HD].T
-    values[0, :HD] = kv_ref[y, HD:]
 
     def arrive(c):
         d_copy(kv_in.at[c], c).wait_recv()
@@ -227,23 +287,34 @@
         t_copy(index, core).wait_send()
         t_copy(index, 1 - core).wait_recv()
     w_local.wait()
+    for k in range(2):
+        for j in range(2):
+            f_copy(k, j).wait_send()
+        for step in (1, 3):
+            g_copy(k, step).wait_send()
+        for j in range(4):
+            h_copy(k, j, core).wait_send()
+            h_copy(k, j, 1 - core).wait_recv()
     for step in (1, 3, 2):
         o_wait(step).wait_recv()
 
 
-def attend(query, kv, w_out, padded, n_tensor):
+def attend(query, kv, w_out, w_up, w_down, padded, n_tensor):
     heads, width, rows = query.shape
     dma = lambda n: pltpu.SemaphoreType.DMA((n,))
     vmem = pl.BlockSpec(memory_space=pltpu.VMEM)
+    hbm = pl.BlockSpec(memory_space=pl.ANY)
     return pl.pallas_call(
         attend_kernel,
-        in_specs=[vmem, vmem, vmem],
-        out_specs=[vmem, pl.BlockSpec(memory_space=pl.ANY)],
+        in_specs=[vmem, vmem, hbm, hbm, hbm],
+        out_specs=[vmem, hbm, hbm, hbm],
         out_shape=[
             jax.ShapeDtypeStruct((heads, width, padded), BF16),
             jax.ShapeDtypeStruct((n_tensor, *w_out.shape), BF16),
+            *(jax.ShapeDtypeStruct((2 * RING, w.shape[0] // (2 * RING), w.shape[1]), BF16) for w in (w_up, w_down)),
         ],
         scratch_shapes=[
+            pltpu.VMEM(w_out.shape, BF16),
             pltpu.VMEM((heads, width, rows), BF16),
             pltpu.VMEM((BLOCKS, 2 * width, rows), BF16),
             pltpu.VMEM((BLOCKS, rows, width), BF16),
@@ -253,13 +324,14 @@
             pltpu.VMEM((2, rows + 8, rows), F32),
             pltpu.VMEM((heads, width, padded), BF16),
             dma(RING), dma(RING), dma(RING), dma(BLOCKS), dma(BLOCKS), dma(BLOCKS), dma(RING), dma(RING),
-            dma(7), dma(7), dma(7), dma(7), dma(1),
+            dma(7), dma(7), dma(7), dma(7), dma(2),
+            dma(4), dma(4), dma(4), dma(4), dma(8), dma(8),
         ],
         cost_estimate=pl.CostEstimate(flops=40 * 10**9, bytes_accessed=8 << 20, transcendentals=0),
         compiler_params=pltpu.CompilerParams(
             vmem_limit_bytes=40 << 20, collective_id=0, has_side_effects=True
         ),
-    )(query, kv, w_out)
+    )(query, kv, w_out, w_up, w_down)
 
 
 class Tensor:
@@ -324,20 +396,58 @@
         copy(name).wait_send()
 
 
-def gather_kernel(x_ref, out_ref, send_sem, recv_sem):
+def heads_kernel(x_ref, out_ref, send_sem, recv_sem):
     t = Tensor()
+    width = x_ref.shape[1] // 2
+    cut = x_ref.shape[0] // 2
+    lo, hi = pl.ds(0, cut), pl.ds(cut, cut)
+    part = lambda plane: x_ref.at[:, pl.ds(pl.multiple_of(plane * width, width), width)]
+    there = 1 - t.plane
     t.meet()
-    out_ref[t.me] = x_ref[...]
-    gather(t, x_ref, out_ref, x_ref.shape[0] // 2, send_sem, recv_sem)
+
+    def copy(src, block, rows, to, i):
+        dst = out_ref.at[block] if rows is None else out_ref.at[block, rows]
+        return send(dst if src is None else src, dst, send_sem.at[i], recv_sem.at[i], to)
+
+    copies = [
+        copy(part(t.plane), t.me, None, t.right, 0),
+        copy(part(t.plane), t.me, None, t.left, 1),
+        copy(part(there), t.me, None, t.pair, 2),
+        copy(None, t.left, lo, t.right, 3),
+        copy(None, t.right, hi, t.left, 4),
+        copy(None, t.pair, None, t.right, 5),
+        copy(None, t.pair, None, t.left, 6),
+        copy(None, t.on(there, 3), lo, t.right, 7),
+        copy(None, t.on(there, 1), hi, t.left, 8),
+    ]
+    for i in (2, 0, 1):
+        copies[i].start()
+    out_ref[t.me] = x_ref[:, pl.ds(pl.multiple_of(t.plane * width, width), width)]
+    copies[2].wait_recv()
+    copies[5].start()
+    copies[6].start()
+    copies[0].wait_recv()
+    copies[3].start()
+    copies[1].wait_recv()
+    copies[4].start()
+    copies[5].wait_recv()
+    copies[7].start()
+    copies[6].wait_recv()
+    copies[8].start()
+    for i in (3, 4, 7, 8):
+        copies[i].wait_recv()
+    for one in copies:
+        one.wait_send()
 
 
 def gather_heads(x, n_tensor):
     dma = lambda n: pltpu.SemaphoreType.DMA((n,))
+    vmem = pl.BlockSpec(memory_space=pltpu.VMEM)
     return pl.pallas_call(
-        gather_kernel,
-        in_specs=[pl.BlockSpec(memory_space=pltpu.VMEM)],
-        out_specs=pl.BlockSpec(memory_space=pltpu.VMEM),
-        out_shape=jax.ShapeDtypeStruct((n_tensor, *x.shape), x.dtype),
+        heads_kernel,
+        in_specs=[vmem],
+        out_specs=vmem,
+        out_shape=jax.ShapeDtypeStruct((n_tensor, x.shape[0], x.shape[1] // 2), x.dtype),
         scratch_shapes=[dma(9), dma(9)],
         cost_estimate=pl.CostEstimate(flops=20 * 10**9, bytes_accessed=8 << 20, transcendentals=0),
         compiler_params=pltpu.CompilerParams(vmem_limit_bytes=16 << 20, collective_id=1, has_side_effects=True),
@@ -345,14 +455,15 @@
 
 
 def finish_kernel(
-    term_ref, mixed_ref, out_ref, own, far_in, over_in, half_in, edge_in, pair_in, far_sum, over_sum, edge_sum,
-    s_send, s_recv, g_send, g_recv,
+    term_ref, mixed_ref, out_ref, base, own, half_in, edge_in, edge_sum, s_send, s_recv, g_send, g_recv, load_sem
 ):
     t = Tensor()
-    part = mixed_ref.shape[0]
+    part = own.shape[0]
     cut = part // 2
     lo, hi = pl.ds(0, cut), pl.ds(cut, cut)
-    there = 1 - t.plane
+    right, left, far = (lax.rem(t.x + step, RING) for step in (1, 3, 2))
+    load = pltpu.make_async_copy(mixed_ref.at[t.x], base, load_sem.at[0])
+    load.start()
     t.meet()
     copies = {}
 
@@ -362,57 +473,41 @@
         copies[name].start()
 
     wait = lambda name: copies[name].wait_recv()
-    far, far_over = t.on(t.plane, 2), t.on(there, 2)
-    go("far", term_ref.at[far_over], far_in, t.pair)
-    go("over right", term_ref.at[t.on(there, 1)], over_in.at[0], t.right)
-    go("over left", term_ref.at[t.on(there, 3)], over_in.at[1], t.left)
-    go("edge right", term_ref.at[t.right, lo], edge_in.at[0, lo], t.right)
-    go("edge left", term_ref.at[t.left, hi], edge_in.at[1, hi], t.left)
-    wait("far")
-    far_sum[...] = (far_in[...].astype(F32) + term_ref[far].astype(F32)).astype(BF16)
-    go("half left", far_sum.at[lo], half_in.at[0], t.left)
-    go("half right", far_sum.at[hi], half_in.at[1], t.right)
-    wait("over right")
-    wait("over left")
-    over_sum[...] = (
-        over_in[0].astype(F32) + over_in[1].astype(F32) + term_ref[t.pair].astype(F32)
-    ).astype(BF16)
-    go("pair", over_sum, pair_in, t.pair)
+    go("half left", term_ref.at[far, lo], half_in.at[0], t.left)
+    go("half right", term_ref.at[far, hi], half_in.at[1], t.right)
+    go("edge right", term_ref.at[right, lo], edge_in.at[0, lo], t.right)
+    go("edge left", term_ref.at[left, hi], edge_in.at[1, hi], t.left)
+    load.wait()
+    base[...] += term_ref[t.x].astype(F32)
     wait("half left")
-    edge_sum[0] = (half_in[0].astype(F32) + term_ref[t.left, lo].astype(F32)).astype(BF16)
+    edge_sum[0] = (half_in[0].astype(F32) + term_ref[left, lo].astype(F32)).astype(BF16)
     go("sum left", edge_sum.at[0], edge_in.at[1, lo], t.left)
     wait("half right")
-    edge_sum[1] = (half_in[1].astype(F32) + term_ref[t.right, hi].astype(F32)).astype(BF16)
+    edge_sum[1] = (half_in[1].astype(F32) + term_ref[right, hi].astype(F32)).astype(BF16)
     go("sum right", edge_sum.at[1], edge_in.at[0, hi], t.right)
-    for name in ("edge right", "edge left", "sum left", "sum right", "pair"):
+    for name in ("edge right", "edge left", "sum left", "sum right"):
         wait(name)
-    own[...] = (
-        mixed_ref[...]
-        + term_ref[t.me].astype(F32)
-        + edge_in[0].astype(F32)
-        + edge_in[1].astype(F32)
-        + pair_in[...].astype(F32)
-    ).astype(BF16)
+    own[...] = (base[...] + edge_in[0].astype(F32) + edge_in[1].astype(F32)).astype(BF16)
     out_ref[t.me] = own[...]
     for name in copies:
         copies[name].wait_send()
     gather(t, own, out_ref, cut, g_send, g_recv)
 
 
-def finish(term, mixed):
-    n_tensor, part, model = term.shape
+def finish(term, mixed, n_tensor):
+    ring, part, model = term.shape
     dma = lambda n: pltpu.SemaphoreType.DMA((n,))
     vmem = pl.BlockSpec(memory_space=pltpu.VMEM)
-    block = lambda *lead: pltpu.VMEM((*lead, part, model), BF16)
     half = pltpu.VMEM((2, part // 2, model), BF16)
     return pl.pallas_call(
         finish_kernel,
-        in_specs=[vmem, vmem],
+        in_specs=[vmem, pl.BlockSpec(memory_space=pl.ANY)],
         out_specs=vmem,
-        out_shape=jax.ShapeDtypeStruct(term.shape, BF16),
+        out_shape=jax.ShapeDtypeStruct((n_tensor, part, model), BF16),
         scratch_shapes=[
-            block(), block(), block(2), half, block(2), block(), block(), block(), half,
-            dma(10), dma(10), dma(9), dma(9),
+            pltpu.VMEM((part, model), F32), pltpu.VMEM((part, model), BF16),
+            half, pltpu.VMEM((2, part, model), BF16), half,
+            dma(6), dma(6), dma(9), dma(9), dma(1),
         ],
         cost_estimate=pl.CostEstimate(flops=40 * 10**9, bytes_accessed=8 << 20, transcendentals=0),
         compiler_params=pltpu.CompilerParams(vmem_limit_bytes=32 << 20, collective_id=2, has_side_effects=True),
@@ -434,16 +529,19 @@
     ).reshape(3, heads, HD, rows)
     query = (qkv[0] * (LOG2E / HD**0.5)).astype(BF16)
     kv = jnp.concatenate([qkv[1], qkv[2]], axis=1).astype(BF16)
-    attended, w_out_all = attend(query, kv, w_out, padded, n_tensor)
-    attended = gather_heads(attended.reshape(span, padded), n_tensor).reshape(n_tensor * span, padded)
-    mixed = jnp.pad(base, ((0, padded - rows), (0, 0))) + lax.dot_general(
+    attended, w_out_all, up_pair, down_pair = attend(query, kv, w_out, w_up, w_down, padded, n_tensor)
+    attended = gather_heads(attended.reshape(span, padded), n_tensor).reshape(n_tensor * span, padded // 2)
+    plane = me // RING
+    base = jnp.pad(tokens, ((0, padded - rows), (0, 0)))
+    base = lax.dynamic_slice_in_dim(base, plane * (padded // 2), padded // 2, 0)
+    mixed = base.astype(F32) + lax.dot_general(
         attended, w_out_all.reshape(n_tensor * span, model), (((0,), (0,)), ((), ())), preferred_element_type=F32
     )
     post = layer_norm(mixed, post_gain).astype(BF16)
-    hidden = jax.nn.gelu(dot(post, w_up), approximate=True).astype(BF16)
-    term = dot(hidden, w_down).astype(BF16).reshape(n_tensor, part, model)
-    own = lax.dynamic_slice_in_dim(mixed, me * part, part, 0)
-    return finish(term, own).reshape(padded, model)[:rows]
+    wide = lambda w: jax.nn.gelu(dot(post, w), approximate=True).astype(BF16)
+    term = dot(wide(w_up), w_down) + dot(wide(up_pair.reshape(w_up.shape)), down_pair.reshape(w_down.shape))
+    term = term.astype(BF16).reshape(RING, part, model)
+    return finish(term, mixed.reshape(RING, part, model), n_tensor).reshape(padded, model)[:rows]
 
 
 def solution(mesh):

time: 140 us -> 133 us (0.950)
  Pallas kernels: 113 us -> 104 us
  matrix products: 15.1 us -> 17.2 us
    pallas_call x3, Pallas kernels: 113 us -> 104 us  [the longest x1 55.6 us: attend(): pl.pallas_call(attend_kernel, in_specs=[vmem, vmem, hbm, hbm, hbm], out_s...]
    dot_general x1 -> x2, matrix products: 9.34 us -> 13.3 us  [dot(): return jnp.dot(a, b, preferred_element_type=F32)]
    dot_general x1, matrix products: 4.12 us -> 2.17 us  [per_device(): lax.dot_general(attended, w_out_all.reshape(n_tensor * span, model), (((0...]
    unnamed x16 -> x24, local copies, waits for them, and re-layouts: 4.35 us -> 6.29 us
where the time goes in v3:
time: 133 us
  Pallas kernels  104 us (78%)
  matrix products  17.2 us (13%)
  local copies, waits for them, and re-layouts  7.83 us (6%)
  other arithmetic  3.34 us (3%)
    pallas_call x1, Pallas kernels, attend(): pl.pallas_call(attend_kernel, in_specs=[vmem, vmem, hbm, hbm, hbm], out_s...  55.6 us
    pallas_call x1, Pallas kernels, finish(): pl.pallas_call(finish_kernel, in_specs=[vmem, pl.BlockSpec(memory_space=p...  32.9 us
    pallas_call x1, Pallas kernels, gather_heads(): pl.pallas_call(heads_kernel, in_specs=[vmem], out_specs=vmem, out_shape=j...  15.5 us
    dot_general x2, matrix products, dot(): return jnp.dot(a, b, preferred_element_type=F32)  13.3 us
    unnamed x24, local copies, waits for them, and re-layouts  6.29 us

profile of v3, /device:TPU:0, one launch (start us, length us, event | category | flops | bytes accessed | tf_op | source)
XLA Modules:
  0.0 132.6 jit_solution(14667309729598930160)
XLA Ops:
  0.0 0.0 copy-start
  0.0 0.0 copy-start.10
  0.0 1.5 %copy-done = bf16[1536,3,192]{0,2,1:T(8,128)(2,1)S(1)} copy-done((bf16[1536,3,192]{0,2,1:T(8,128)(2,1)S(1)}, bf16[1536,3,192]{0,2,1:T(8,128)(2,1)}, u32[]{:S(2)}) %copy-start) | copy-done | bytes 1769496
  1.5 0.0 copy-start.8
  1.5 2.1 %convert_reduce_fusion = f32[720]{0:T(1024)S(1)} fusion(bf16[720,1536]{1,0:T(8,128)(2,1)} %param.7), kind=kLoop, calls=%fused_computation.1 | loop fusion | flops 2211120 | bytes 2214720 | tf_op jit(solution)/shard_map/reduce_sum | solution.py:20
  3.6 0.1 copy-done.8
  3.8 0.7 fusion.2
  4.5 0.0 copy-done.10
  4.5 0.0 copy-start.4
  4.5 1.7 %fusion.54 = (bf16[576,720]{1,0:T(8,128)(2,1)S(1)}, f32[576,720]{1,0:T(8,128)S(1)}) fusion(bf16[1536,576]{0,1:T(8,128)(2,1)S(1)} %bitcast.23, bf16[720,1536]{1,0:T(8,128)(2,1)S(1)} %copy-done.8, f32[1536]{0:T(1024)S(1)} %copy-done.10, f32[720]{0:T(1024)S(1)} %add_rsqrt_fusion, f32[720]{0:T(1024)S(1)} %broadcast_multiply_fusion), kind=kOutput, calls=%fused_computation.64 | convolution fusion | flops 1279964160 | bytes 6481536 | tf_op jit(solution)/shard_map/dot_general | solution.py:527
  6.2 0.0 copy-start.3
  6.2 0.0 copy-start.5
  6.3 0.1 pad_maximum_fusion.kv_ref
  6.4 0.0 copy-done.4
  6.4 1.5 %copy-done.3 = bf16[768,1536]{1,0:T(8,128)(2,1)S(1)} copy-done((bf16[768,1536]{1,0:T(8,128)(2,1)S(1)}, bf16[768,1536]{1,0:T(8,128)(2,1)}, u32[]{:S(2)}) %copy-start.3) | copy-done | bytes 2359320
  7.9 0.1 copy-done.5
  8.0 55.6 %shard_map.73 = (bf16[4,48,768]{2,1,0:T(8,128)(2,1)S(1)}, bf16[8,192,1536]{2,1,0:T(8,128)(2,1)}, bf16[8,192,768]{2,1,0:T(8,128)(2,1)S(1)}, bf16[8,96,1536]{2,1,0:T(8,128)(2,1)S(1)}) custom-call(bf16[4,48,720]{2,1,0:T(8,128)(2,1)S(1)} %bitcast.26, bf16[4,96,720]{2,1,0:T(8,128)(2,1)S(1)} %pad_maximum_fusion.kv_ref, bf16[192,1536]{1,0:T(8,128)(2,1)S(1)} %copy-done.5, ...), custom_call_target="tpu_custom_call" | custom-call | flops 40000000000 | bytes 8388608 | tf_op jit(solution)/shard_map/pallas_call | solution.py:307
  63.5 0.0 copy-start.6
  63.5 0.0 copy-start.7
  63.6 0.0 copy-start.9
  63.6 15.5 %shard_map.74 = bf16[8,192,384]{2,1,0:T(8,128)(2,1)S(1)} custom-call(bf16[192,768]{1,0:T(8,128)(2,1)S(1)} %bitcast.30), custom_call_target="tpu_custom_call" | custom-call | flops 20000000000 | bytes 8388608 | tf_op jit(solution)/shard_map/pallas_call | solution.py:446
  79.1 0.0 copy-done.6
  79.1 0.0 copy-done.7
  79.1 0.0 copy-done.9
  79.1 2.2 %fusion.55 = (f32[384]{0:T(512)S(1)}, f32[384,1536]{1,0:T(8,128)S(1)}) fusion(bf16[8,192,384]{2,1,0:T(8,128)(2,1)S(1)} %shard_map.74, bf16[8,192,1536]{2,1,0:T(8,128)(2,1)S(1)} %copy-done.9, s32[]{:T(128)S(6)} %select_n.9, bf16[720,1536]{1,0:T(8,128)(2,1)S(1)} %copy-done.8), kind=kOutput, calls=%fused_computation.65 | convolution fusion | flops 1813708416 | bytes 10470916 | tf_op jit(solution)/shard_map/dot_general | solution.py:537
  81.3 0.0 copy-start.1
  81.3 0.0 copy-start.11
  81.3 1.4 %copy-done.1 = f32[384,1536]{1,0:T(8,128)} copy-done((f32[384,1536]{1,0:T(8,128)}, f32[384,1536]{1,0:T(8,128)S(1)}, u32[]{:S(2)}) %copy-start.1) | copy-done | bytes 2359320
  82.7 0.4 multiply_reduce_fusion
  83.1 0.0 copy-done.11
  83.1 7.0 %fusion.32 = f32[384,1536]{1,0:T(8,128)} fusion(bf16[768,1536]{1,0:T(8,128)(2,1)} %down_ref.1, bf16[1536,768]{1,0:T(8,128)(2,1)} %up_ref.1, f32[384,1536]{1,0:T(8,128)} %copy-done.1, f32[1536]{0:T(1024)S(1)} %copy-done.11, f32[384]{0:T(512)S(1)} %add_rsqrt_fusion.1, f32[384]{0:T(512)S(1)} %broadcast_multiply_fusion.1), kind=kOutput, calls=%fused_computation.37 | convolution fusion | flops 1816952832 | bytes 9446400 | tf_op jit(solution)/shard_map/dot_general | solution.py:27
  90.2 6.3 %fusion.6 = bf16[384,1536]{1,0:T(8,128)(2,1)S(1)} fusion(f32[384,1536]{1,0:T(8,128)} %fusion.32, bf16[768,1536]{1,0:T(8,128)(2,1)} %bitcast.28, bf16[1536,768]{1,0:T(8,128)(2,1)} %bitcast.27, f32[384,1536]{1,0:T(8,128)} %copy-done.1, f32[1536]{0:T(1024)S(1)} %copy-done.11, f32[384]{0:T(512)S(1)} %add_rsqrt_fusion.1, f32[384]{0:T(512)S(1)} %broadcast_multiply_fusion.1), kind=kOutput, calls=%fused_computation.10 | convolution fusion | flops 1818132480 | bytes 10626048 | tf_op jit(solution)/shard_map/dot_general | solution.py:27
  96.5 0.0 copy-start.2
  96.5 1.7 %copy-done.2 = f32[384,1536]{1,0:T(8,128)S(1)} copy-done((f32[384,1536]{1,0:T(8,128)S(1)}, f32[384,1536]{1,0:T(8,128)}, u32[]{:S(2)}) %copy-start.2) | copy-done | bytes 2359320
  98.1 32.9 %shard_map.75 = bf16[8,96,1536]{2,1,0:T(8,128)(2,1)S(1)} custom-call(bf16[4,96,1536]{2,1,0:T(8,128)(2,1)S(1)} %bitcast.29, f32[4,96,1536]{2,1,0:T(8,128)S(1)} %bitcast.24), custom_call_target="tpu_custom_call" | custom-call | flops 40000000000 | bytes 8388608 | tf_op jit(solution)/shard_map/pallas_call | solution.py:502
  131.1 1.5 %slice.24 = bf16[720,1536]{1,0:T(8,128)(2,1)} slice(bf16[768,1536]{1,0:T(8,128)(2,1)S(1)} %bitcast.25), slice={[0:720], [0:1536]} | slice | bytes 4423680 | tf_op jit(solution)/shard_map/slice | solution.py:544
  (6 shorter events, 0.1 us)
Async XLA Ops:
  0.0 1.5 %copy-start = (bf16[1536,3,192]{0,2,1:T(8,128)(2,1)S(1)}, bf16[1536,3,192]{0,2,1:T(8,128)(2,1)}, u32[]{:S(2)}) copy-start(bf16[1536,3,192]{0,2,1:T(8,128)(2,1)} %param.9) | copy-start | bytes 5308420
  0.0 4.5 %copy-start.10 = (f32[1536]{0:T(1024)S(1)}, f32[1536]{0:T(1024)}, u32[]{:S(2)}) copy-start(f32[1536]{0:T(1024)} %param.8) | copy-start | bytes 18436
  1.5 2.3 %copy-start.8 = (bf16[720,1536]{1,0:T(8,128)(2,1)S(1)}, bf16[720,1536]{1,0:T(8,128)(2,1)}, u32[]{:S(2)}) copy-start(bf16[720,1536]{1,0:T(8,128)(2,1)} %param.7) | copy-start | bytes 6635524
  4.5 1.9 %copy-start.4 = (bf16[1536,768]{1,0:T(8,128)(2,1)S(1)}, bf16[1536,768]{1,0:T(8,128)(2,1)}, u32[]{:S(2)}) copy-start(bf16[1536,768]{1,0:T(8,128)(2,1)} %up_ref.1) | copy-start | bytes 7077892
  6.2 1.7 %copy-start.3 = (bf16[768,1536]{1,0:T(8,128)(2,1)S(1)}, bf16[768,1536]{1,0:T(8,128)(2,1)}, u32[]{:S(2)}) copy-start(bf16[768,1536]{1,0:T(8,128)(2,1)} %down_ref.1) | copy-start | bytes 7077892
  6.2 1.8 %copy-start.5 = (bf16[192,1536]{1,0:T(8,128)(2,1)S(1)}, bf16[192,1536]{1,0:T(8,128)(2,1)}, u32[]{:S(2)}) copy-start(bf16[192,1536]{1,0:T(8,128)(2,1)} %w_hbm.1) | copy-start | bytes 1769476
  63.5 15.6 %copy-start.6 = (bf16[8,192,768]{2,1,0:T(8,128)(2,1)}, bf16[8,192,768]{2,1,0:T(8,128)(2,1)S(1)}, u32[]{:S(2)}) copy-start(bf16[8,192,768]{2,1,0:T(8,128)(2,1)S(1)} %get-tuple-element.11) | copy-start | bytes 7077892
  63.5 15.6 %copy-start.7 = (bf16[8,96,1536]{2,1,0:T(8,128)(2,1)}, bf16[8,96,1536]{2,1,0:T(8,128)(2,1)S(1)}, u32[]{:S(2)}) copy-start(bf16[8,96,1536]{2,1,0:T(8,128)(2,1)S(1)} %get-tuple-element.12) | copy-start | bytes 7077892
  63.6 15.6 %copy-start.9 = (bf16[8,192,1536]{2,1,0:T(8,128)(2,1)S(1)}, bf16[8,192,1536]{2,1,0:T(8,128)(2,1)}, u32[]{:S(2)}) copy-start(bf16[8,192,1536]{2,1,0:T(8,128)(2,1)} %get-tuple-element.10) | copy-start | bytes 14155780
  81.3 1.4 %copy-start.1 = (f32[384,1536]{1,0:T(8,128)}, f32[384,1536]{1,0:T(8,128)S(1)}, u32[]{:S(2)}) copy-start(f32[384,1536]{1,0:T(8,128)S(1)} %get-tuple-element.18) | copy-start | bytes 7077892
  81.3 1.8 %copy-start.11 = (f32[1536]{0:T(1024)S(1)}, f32[1536]{0:T(1024)}, u32[]{:S(2)}) copy-start(f32[1536]{0:T(1024)} %param.11) | copy-start | bytes 18436
  96.5 1.7 %copy-start.2 = (f32[384,1536]{1,0:T(8,128)S(1)}, f32[384,1536]{1,0:T(8,128)}, u32[]{:S(2)}) copy-start(f32[384,1536]{1,0:T(8,128)} %copy-done.1) | copy-start | bytes 7077892

commit v4 on v3

--- a/solution.py
+++ b/solution.py
@@ -303,7 +303,7 @@
     heads, width, rows = query.shape
     dma = lambda n: pltpu.SemaphoreType.DMA((n,))
     vmem = pl.BlockSpec(memory_space=pltpu.VMEM)
-    hbm = pl.BlockSpec(memory_space=pl.ANY)
+    hbm = pl.BlockSpec(memory_space=pltpu.HBM)
     return pl.pallas_call(
         attend_kernel,
         in_specs=[vmem, vmem, hbm, hbm, hbm],
@@ -396,23 +396,52 @@
         copy(name).wait_send()
 
 
-def heads_kernel(x_ref, out_ref, send_sem, recv_sem):
+def tail_kernel(
+    heads_ref, tokens_hbm, gain_ref, w_hbm, up_hbm, up_pair_hbm, down_hbm, down_pair_hbm, out_ref,
+    heads, w_out, up, down, tokens, mixed, term, own, half_in, edge_in, edge_sum,
+    a_send, a_recv, s_send, s_recv, g_send, g_recv, load_sem,
+):
     t = Tensor()
-    width = x_ref.shape[1] // 2
-    cut = x_ref.shape[0] // 2
+    half, model = mixed.shape
+    part = half // RING
+    there = 1 - t.plane
+    valid = tokens_hbm.shape[0] - half
+    loads = [
+        pltpu.make_async_copy(w_hbm, w_out, load_sem.at[0]),
+        pltpu.make_async_copy(up_hbm, up.at[0], load_sem.at[1]),
+        pltpu.make_async_copy(up_pair_hbm, up.at[1], load_sem.at[2]),
+        pltpu.make_async_copy(down_hbm, down.at[0], load_sem.at[3]),
+        pltpu.make_async_copy(down_pair_hbm, down.at[1], load_sem.at[4]),
+    ]
+    first = pltpu.make_async_copy(tokens_hbm.at[pl.ds(0, half)], tokens, load_sem.at[5])
+    second = pltpu.make_async_copy(tokens_hbm.at[pl.ds(half, valid)], tokens.at[pl.ds(0, valid)], load_sem.at[5])
+
+    @pl.when(t.plane == 0)
+    def _():
+        first.start()
+
+    @pl.when(t.plane == 1)
+    def _():
+        second.start()
+        tokens[valid:] = jnp.zeros((half - valid, model), BF16)
+
+    for load in loads:
+        load.start()
+    t.meet()
+
+    cut = heads_ref.shape[0] // 2
     lo, hi = pl.ds(0, cut), pl.ds(cut, cut)
-    part = lambda plane: x_ref.at[:, pl.ds(pl.multiple_of(plane * width, width), width)]
-    there = 1 - t.plane
-    t.meet()
+    lanes = lambda plane: pl.ds(pl.multiple_of(plane * half, half), half)
 
     def copy(src, block, rows, to, i):
-        dst = out_ref.at[block] if rows is None else out_ref.at[block, rows]
-        return send(dst if src is None else src, dst, send_sem.at[i], recv_sem.at[i], to)
-
+        dst = heads.at[block] if rows is None else heads.at[block, rows]
+        return send(dst if src is None else src, dst, a_send.at[i], a_recv.at[i], to)
+
+    mine, theirs = heads_ref.at[:, lanes(t.plane)], heads_ref.at[:, lanes(there)]
     copies = [
-        copy(part(t.plane), t.me, None, t.right, 0),
-        copy(part(t.plane), t.me, None, t.left, 1),
-        copy(part(there), t.me, None, t.pair, 2),
+        copy(mine, t.me, None, t.right, 0),
+        copy(mine, t.me, None, t.left, 1),
+        copy(theirs, t.me, None, t.pair, 2),
         copy(None, t.left, lo, t.right, 3),
         copy(None, t.right, hi, t.left, 4),
         copy(None, t.pair, None, t.right, 5),
@@ -422,96 +451,120 @@
     ]
     for i in (2, 0, 1):
         copies[i].start()
-    out_ref[t.me] = x_ref[:, pl.ds(pl.multiple_of(t.plane * width, width), width)]
-    copies[2].wait_recv()
-    copies[5].start()
-    copies[6].start()
-    copies[0].wait_recv()
-    copies[3].start()
-    copies[1].wait_recv()
-    copies[4].start()
-    copies[5].wait_recv()
-    copies[7].start()
-    copies[6].wait_recv()
-    copies[8].start()
-    for i in (3, 4, 7, 8):
-        copies[i].wait_recv()
-    for one in copies:
-        one.wait_send()
-
-
-def gather_heads(x, n_tensor):
-    dma = lambda n: pltpu.SemaphoreType.DMA((n,))
-    vmem = pl.BlockSpec(memory_space=pltpu.VMEM)
-    return pl.pallas_call(
-        heads_kernel,
-        in_specs=[vmem],
-        out_specs=vmem,
-        out_shape=jax.ShapeDtypeStruct((n_tensor, x.shape[0], x.shape[1] // 2), x.dtype),
-        scratch_shapes=[dma(9), dma(9)],
-        cost_estimate=pl.CostEstimate(flops=20 * 10**9, bytes_accessed=8 << 20, transcendentals=0),
-        compiler_params=pltpu.CompilerParams(vmem_limit_bytes=16 << 20, collective_id=1, has_side_effects=True),
-    )(x)
-
-
-def finish_kernel(
-    term_ref, mixed_ref, out_ref, base, own, half_in, edge_in, edge_sum, s_send, s_recv, g_send, g_recv, load_sem
-):
-    t = Tensor()
-    part = own.shape[0]
+    heads[t.me] = heads_ref[:, lanes(t.plane)]
+
+    @pl.when(t.plane == 0)
+    def _():
+        first.wait()
+
+    @pl.when(t.plane == 1)
+    def _():
+        second.wait()
+
+    mixed[...] = tokens[...].astype(F32)
+    loads[0].wait()
+
+    def group(i, carry):
+        for when, waits, starts in (
+            (1, (2,), (5, 6)),
+            (2, (0,), (3,)),
+            (3, (1, 5), (4, 7)),
+            (4, (6,), (8,)),
+            (6, (3, 4), ()),
+            (7, (7, 8), ()),
+        ):
+            @pl.when(i == when)
+            def _():
+                for one in waits:
+                    copies[one].wait_recv()
+                for one in starts:
+                    copies[one].start()
+
+        step = lax.rem(3 * (i // 2) * (i // 2 + 1) // 2, RING)
+        side = lax.rem(t.plane + i, 2)
+        who = side * RING + lax.rem(t.x + step, RING)
+        mixed[...] += lax.dot_general(
+            heads[who], w_out[who], (((0,), (0,)), ((), ())), preferred_element_type=F32
+        )
+        return carry
+
+    lax.fori_loop(0, 2 * RING, group, 0)
+    for load in loads[1:]:
+        load.wait()
+
     cut = part // 2
     lo, hi = pl.ds(0, cut), pl.ds(cut, cut)
     right, left, far = (lax.rem(t.x + step, RING) for step in (1, 3, 2))
-    load = pltpu.make_async_copy(mixed_ref.at[t.x], base, load_sem.at[0])
-    load.start()
-    t.meet()
-    copies = {}
-
-    def go(name, src, dst, to):
-        i = len(copies)
-        copies[name] = send(src, dst, s_send.at[i], s_recv.at[i], to)
-        copies[name].start()
-
-    wait = lambda name: copies[name].wait_recv()
-    go("half left", term_ref.at[far, lo], half_in.at[0], t.left)
-    go("half right", term_ref.at[far, hi], half_in.at[1], t.right)
-    go("edge right", term_ref.at[right, lo], edge_in.at[0, lo], t.right)
-    go("edge left", term_ref.at[left, hi], edge_in.at[1, hi], t.left)
-    load.wait()
-    base[...] += term_ref[t.x].astype(F32)
-    wait("half left")
-    edge_sum[0] = (half_in[0].astype(F32) + term_ref[left, lo].astype(F32)).astype(BF16)
-    go("sum left", edge_sum.at[0], edge_in.at[1, lo], t.left)
-    wait("half right")
-    edge_sum[1] = (half_in[1].astype(F32) + term_ref[right, hi].astype(F32)).astype(BF16)
-    go("sum right", edge_sum.at[1], edge_in.at[0, hi], t.right)
-    for name in ("edge right", "edge left", "sum left", "sum right"):
-        wait(name)
-    own[...] = (base[...] + edge_in[0].astype(F32) + edge_in[1].astype(F32)).astype(BF16)
+
+    def sums(src, dst, i, to):
+        return send(src, dst, s_send.at[i], s_recv.at[i], to)
+
+    half_left = sums(term.at[far, lo], half_in.at[0], 0, t.left)
+    half_right = sums(term.at[far, hi], half_in.at[1], 1, t.right)
+    edge_right = sums(term.at[right, lo], edge_in.at[0, lo], 2, t.right)
+    edge_left = sums(term.at[left, hi], edge_in.at[1, hi], 3, t.left)
+    sum_left = sums(edge_sum.at[0], edge_in.at[1, lo], 4, t.left)
+    sum_right = sums(edge_sum.at[1], edge_in.at[0, hi], 5, t.right)
+    rows_of = lambda b: pl.ds(pl.multiple_of(b * part, part), part)
+
+    def feed(i, carry):
+        b = lax.rem(t.x + 2 + 3 * i * (i + 1) // 2, RING)
+        post = layer_norm(mixed[rows_of(b)], gain_ref[...]).astype(BF16)
+        wide = lambda k: jax.nn.gelu(dot(post, up[k]), approximate=True).astype(BF16)
+        term[b] = (dot(wide(0), down[0]) + dot(wide(1), down[1])).astype(BF16)
+        for when, starts in ((0, (half_left, half_right)), (1, (edge_right,)), (2, (edge_left,))):
+            @pl.when(i == when)
+            def _():
+                for one in starts:
+                    one.start()
+        return carry
+
+    lax.fori_loop(0, RING, feed, 0)
+    half_left.wait_recv()
+    edge_sum[0] = (half_in[0].astype(F32) + term[left, lo].astype(F32)).astype(BF16)
+    sum_left.start()
+    half_right.wait_recv()
+    edge_sum[1] = (half_in[1].astype(F32) + term[right, hi].astype(F32)).astype(BF16)
+    sum_right.start()
+    base = mixed[rows_of(t.x)] + term[t.x].astype(F32)
+    mixed[rows_of(t.x)] = base
+    for one in (edge_right, edge_left, sum_left, sum_right):
+        one.wait_recv()
+    own[...] = (mixed[rows_of(t.x)] + edge_in[0].astype(F32) + edge_in[1].astype(F32)).astype(BF16)
     out_ref[t.me] = own[...]
-    for name in copies:
-        copies[name].wait_send()
+    for one in (*copies, half_left, half_right, edge_right, edge_left, sum_left, sum_right):
+        one.wait_send()
     gather(t, own, out_ref, cut, g_send, g_recv)
 
 
-def finish(term, mixed, n_tensor):
-    ring, part, model = term.shape
+def tail(heads, tokens, gain, w_out, up, up_pair, down, down_pair, part):
+    n_tensor, span, model = w_out.shape
+    half = RING * part
     dma = lambda n: pltpu.SemaphoreType.DMA((n,))
     vmem = pl.BlockSpec(memory_space=pltpu.VMEM)
-    half = pltpu.VMEM((2, part // 2, model), BF16)
+    hbm = pl.BlockSpec(memory_space=pltpu.HBM)
     return pl.pallas_call(
-        finish_kernel,
-        in_specs=[vmem, pl.BlockSpec(memory_space=pl.ANY)],
+        tail_kernel,
+        in_specs=[vmem, hbm, vmem, hbm, hbm, hbm, hbm, hbm],
         out_specs=vmem,
         out_shape=jax.ShapeDtypeStruct((n_tensor, part, model), BF16),
         scratch_shapes=[
-            pltpu.VMEM((part, model), F32), pltpu.VMEM((part, model), BF16),
-            half, pltpu.VMEM((2, part, model), BF16), half,
-            dma(6), dma(6), dma(9), dma(9), dma(1),
+            pltpu.VMEM((n_tensor, span, half), BF16),
+            pltpu.VMEM(w_out.shape, BF16),
+            pltpu.VMEM((2, *up.shape), BF16),
+            pltpu.VMEM((2, *down.shape), BF16),
+            pltpu.VMEM((half, model), BF16),
+            pltpu.VMEM((half, model), F32),
+            pltpu.VMEM((RING, part, model), BF16),
+            pltpu.VMEM((part, model), BF16),
+            pltpu.VMEM((2, part // 2, model), BF16),
+            pltpu.VMEM((2, part, model), BF16),
+            pltpu.VMEM((2, part // 2, model), BF16),
+            dma(9), dma(9), dma(6), dma(6), dma(9), dma(9), dma(6),
         ],
-        cost_estimate=pl.CostEstimate(flops=40 * 10**9, bytes_accessed=8 << 20, transcendentals=0),
-        compiler_params=pltpu.CompilerParams(vmem_limit_bytes=32 << 20, collective_id=2, has_side_effects=True),
-    )(term, mixed)
+        cost_estimate=pl.CostEstimate(flops=60 * 10**9, bytes_accessed=20 << 20, transcendentals=0),
+        compiler_params=pltpu.CompilerParams(vmem_limit_bytes=48 << 20, collective_id=1, has_side_effects=True),
+    )(heads, tokens, gain, w_out, up, up_pair, down, down_pair)
 
 
 def per_device(n_seq, n_tensor, tokens, norm_gain, w_qkv, w_out, post_gain, w_up, w_down):
@@ -520,7 +573,6 @@
     heads = span // HD
     part = -(-rows // (16 * n_tensor)) * 16
     padded = n_tensor * part
-    me = lax.axis_index("tensor")
 
     base = tokens.astype(F32)
     normed = layer_norm(base, norm_gain).astype(BF16)
@@ -530,18 +582,11 @@
     query = (qkv[0] * (LOG2E / HD**0.5)).astype(BF16)
     kv = jnp.concatenate([qkv[1], qkv[2]], axis=1).astype(BF16)
     attended, w_out_all, up_pair, down_pair = attend(query, kv, w_out, w_up, w_down, padded, n_tensor)
-    attended = gather_heads(attended.reshape(span, padded), n_tensor).reshape(n_tensor * span, padded // 2)
-    plane = me // RING
-    base = jnp.pad(tokens, ((0, padded - rows), (0, 0)))
-    base = lax.dynamic_slice_in_dim(base, plane * (padded // 2), padded // 2, 0)
-    mixed = base.astype(F32) + lax.dot_general(
-        attended, w_out_all.reshape(n_tensor * span, model), (((0,), (0,)), ((), ())), preferred_element_type=F32
+    out = tail(
+        attended.reshape(span, padded), tokens, post_gain.reshape(1, model), w_out_all,
+        w_up, up_pair.reshape(w_up.shape), w_down, down_pair.reshape(w_down.shape), part,
     )
-    post = layer_norm(mixed, post_gain).astype(BF16)
-    wide = lambda w: jax.nn.gelu(dot(post, w), approximate=True).astype(BF16)
-    term = dot(wide(w_up), w_down) + dot(wide(up_pair.reshape(w_up.shape)), down_pair.reshape(w_down.shape))
-    term = term.astype(BF16).reshape(RING, part, model)
-    return finish(term, mixed.reshape(RING, part, model), n_tensor).reshape(padded, model)[:rows]
+    return out.reshape(padded, model)[:rows]
 
 
 def solution(mesh):

time: 133 us -> 118 us (0.89)
  matrix products: 17.2 us -> 1.69 us
    dot_general x3 -> x0, matrix products: 15.5 us -> none  [the longest x2 13.3 us: dot(): return jnp.dot(a, b, preferred_element_type=F32)]
    pallas_call x2 -> x1, Pallas kernels: 48.5 us -> 49.2 us  [tail(): pl.pallas_call(tail_kernel, in_specs=[vmem, hbm, vmem, hbm, hbm, hbm, hbm...]
    unnamed x24 -> x18, local copies, waits for them, and re-layouts: 6.29 us -> 5.96 us
where the time goes in v4:
time: 118 us; the launch traced here: 117 us
  Pallas kernels  105 us (89%)
  local copies, waits for them, and re-layouts  7.51 us (6%)
  other arithmetic  2.82 us (2%)
  matrix products  1.69 us (1%)
    pallas_call x1, Pallas kernels, attend(): pl.pallas_call(attend_kernel, in_specs=[vmem, vmem, hbm, hbm, hbm], out_s...  55.6 us
    pallas_call x1, Pallas kernels, tail(): pl.pallas_call(tail_kernel, in_specs=[vmem, hbm, vmem, hbm, hbm, hbm, hbm...  49.2 us
    unnamed x18, local copies, waits for them, and re-layouts  5.96 us

profile of v4, /device:TPU:0, one launch (start us, length us, event | category | flops | bytes accessed | tf_op | source)
XLA Modules:
  0.0 116.9 jit_solution(8799861292356755887)
XLA Ops:
  0.0 0.0 copy-start
  0.0 0.0 copy-start.1
  0.0 0.0 copy-start.7
  0.0 1.5 %copy-done = bf16[1536,3,192]{0,2,1:T(8,128)(2,1)S(1)} copy-done((bf16[1536,3,192]{0,2,1:T(8,128)(2,1)S(1)}, bf16[1536,3,192]{0,2,1:T(8,128)(2,1)}, u32[]{:S(2)}) %copy-start) | copy-done | bytes 1769496
  1.5 0.0 copy-start.8
  1.5 2.0 %convert_reduce_fusion = f32[720]{0:T(1024)S(1)} fusion(bf16[720,1536]{1,0:T(8,128)(2,1)} %tokens_hbm.1), kind=kLoop, calls=%fused_computation.1 | loop fusion | flops 2211120 | bytes 2214720 | tf_op jit(solution)/shard_map/reduce_sum | solution.py:20
  3.5 0.0 copy-done.1
  3.5 0.7 fusion.2
  4.2 0.0 copy-done.7
  4.2 0.0 copy-done.8
  4.3 0.0 copy-start.3
  4.3 1.7 %fusion.15 = (bf16[576,720]{1,0:T(8,128)(2,1)S(1)}, f32[576,720]{1,0:T(8,128)S(1)}) fusion(bf16[1536,576]{0,1:T(8,128)(2,1)S(1)} %bitcast.11, bf16[720,1536]{1,0:T(8,128)(2,1)S(1)} %copy-done.1, f32[1536]{0:T(1024)S(1)} %copy-done.8, f32[720]{0:T(1024)S(1)} %add_rsqrt_fusion, f32[720]{0:T(1024)S(1)} %broadcast_multiply_fusion), kind=kOutput, calls=%fused_computation.18 | convolution fusion | flops 1279964160 | bytes 6481536 | tf_op jit(solution)/shard_map/dot_general | solution.py:579
  6.0 0.0 copy-start.2
  6.0 0.0 copy-start.4
  6.0 0.1 pad_maximum_fusion.kv_ref
  6.2 0.0 copy-done.3
  6.2 1.5 %copy-done.2 = bf16[1536,768]{1,0:T(8,128)(2,1)S(1)} copy-done((bf16[1536,768]{1,0:T(8,128)(2,1)S(1)}, bf16[1536,768]{1,0:T(8,128)(2,1)}, u32[]{:S(2)}) %copy-start.2) | copy-done | bytes 2359320
  7.6 0.1 copy-done.4
  7.7 55.6 %shard_map.73 = (bf16[4,48,768]{2,1,0:T(8,128)(2,1)S(1)}, bf16[8,192,1536]{2,1,0:T(8,128)(2,1)}, bf16[8,192,768]{2,1,0:T(8,128)(2,1)S(1)}, bf16[8,96,1536]{2,1,0:T(8,128)(2,1)S(1)}) custom-call(bf16[4,48,720]{2,1,0:T(8,128)(2,1)S(1)} %bitcast.13, bf16[4,96,720]{2,1,0:T(8,128)(2,1)S(1)} %pad_maximum_fusion.kv_ref, bf16[192,1536]{1,0:T(8,128)(2,1)S(1)} %copy-done.4, ...), custom_call_target="tpu_custom_call" | custom-call | flops 40000000000 | bytes 8388608 | tf_op jit(solution)/shard_map/pallas_call | solution.py:307
  63.3 0.0 copy-start.5
  63.3 1.4 %copy-done.5 = bf16[8,192,768]{2,1,0:T(8,128)(2,1)} copy-done((bf16[8,192,768]{2,1,0:T(8,128)(2,1)}, bf16[8,192,768]{2,1,0:T(8,128)(2,1)S(1)}, u32[]{:S(2)}) %copy-start.5) | copy-done | bytes 2359320
  64.8 0.0 copy-start.6
  64.8 1.5 %copy-done.6 = bf16[8,96,1536]{2,1,0:T(8,128)(2,1)} copy-done((bf16[8,96,1536]{2,1,0:T(8,128)(2,1)}, bf16[8,96,1536]{2,1,0:T(8,128)(2,1)S(1)}, u32[]{:S(2)}) %copy-start.6) | copy-done | bytes 2359320
  66.2 49.2 %shard_map.74 = bf16[8,96,1536]{2,1,0:T(8,128)(2,1)S(1)} custom-call(bf16[192,768]{1,0:T(8,128)(2,1)S(1)} %bitcast.16, bf16[720,1536]{1,0:T(8,128)(2,1)S(1)} %copy-done.1, f32[1,1536]{1,0:T(1,128)S(1)} %reshape.43.gain_ref, bf16[8,192,1536]{2,1,0:T(8,128)(2,1)} %get-tuple-element.10.w_hbm, bf16[1536,768]{1,0:T(8,128)(2,1)} %up_hbm.1, ...), custom_call_target="tpu_custom_call" | custom-call | flops 60000002048 | bytes 20971520 | tf_op jit(solution)/shard_map/pallas_call | solution.py:546
  115.4 1.5 %slice.24 = bf16[720,1536]{1,0:T(8,128)(2,1)} slice(bf16[768,1536]{1,0:T(8,128)(2,1)S(1)} %bitcast.12), slice={[0:720], [0:1536]} | slice | bytes 4423680 | tf_op jit(solution)/shard_map/slice | solution.py:589
  (5 shorter events, 0.1 us)
Async XLA Ops:
  0.0 1.5 %copy-start = (bf16[1536,3,192]{0,2,1:T(8,128)(2,1)S(1)}, bf16[1536,3,192]{0,2,1:T(8,128)(2,1)}, u32[]{:S(2)}) copy-start(bf16[1536,3,192]{0,2,1:T(8,128)(2,1)} %param.9) | copy-start | bytes 5308420
  0.0 3.5 %copy-start.1 = (bf16[720,1536]{1,0:T(8,128)(2,1)S(1)}, bf16[720,1536]{1,0:T(8,128)(2,1)}, u32[]{:S(2)}) copy-start(bf16[720,1536]{1,0:T(8,128)(2,1)} %tokens_hbm.1) | copy-start | bytes 6635524
  0.0 4.2 %copy-start.7 = (f32[1536]{0:T(1024)S(1)}, f32[1536]{0:T(1024)}, u32[]{:S(2)}) copy-start(f32[1536]{0:T(1024)} %param.11) | copy-start | bytes 18436
  1.5 2.8 %copy-start.8 = (f32[1536]{0:T(1024)S(1)}, f32[1536]{0:T(1024)}, u32[]{:S(2)}) copy-start(f32[1536]{0:T(1024)} %param.8) | copy-start | bytes 18436
  4.3 1.9 %copy-start.3 = (bf16[768,1536]{1,0:T(8,128)(2,1)S(1)}, bf16[768,1536]{1,0:T(8,128)(2,1)}, u32[]{:S(2)}) copy-start(bf16[768,1536]{1,0:T(8,128)(2,1)} %down_hbm.1) | copy-start | bytes 7077892
  6.0 1.7 %copy-start.2 = (bf16[1536,768]{1,0:T(8,128)(2,1)S(1)}, bf16[1536,768]{1,0:T(8,128)(2,1)}, u32[]{:S(2)}) copy-start(bf16[1536,768]{1,0:T(8,128)(2,1)} %up_hbm.1) | copy-start | bytes 7077892
  6.0 1.8 %copy-start.4 = (bf16[192,1536]{1,0:T(8,128)(2,1)S(1)}, bf16[192,1536]{1,0:T(8,128)(2,1)}, u32[]{:S(2)}) copy-start(bf16[192,1536]{1,0:T(8,128)(2,1)} %w_hbm.1) | copy-start | bytes 1769476
  63.3 1.4 %copy-start.5 = (bf16[8,192,768]{2,1,0:T(8,128)(2,1)}, bf16[8,192,768]{2,1,0:T(8,128)(2,1)S(1)}, u32[]{:S(2)}) copy-start(bf16[8,192,768]{2,1,0:T(8,128)(2,1)S(1)} %get-tuple-element.11) | copy-start | bytes 7077892
  64.8 1.5 %copy-start.6 = (bf16[8,96,1536]{2,1,0:T(8,128)(2,1)}, bf16[8,96,1536]{2,1,0:T(8,128)(2,1)S(1)}, u32[]{:S(2)}) copy-start(bf16[8,96,1536]{2,1,0:T(8,128)(2,1)S(1)} %get-tuple-element.12) | copy-start | bytes 7077892

commit v5 on v4

--- a/solution.py
+++ b/solution.py
@@ -133,40 +133,25 @@
         @pl.when(c == 5)
         def _():
             for k in range(2):
-                f_copy(k, 1).start()
                 f_copy(k, 0).wait_recv()
                 for step in (1, 3):
                     g_copy(k, step).start()
                 h_copy(k, 0, core).start()
 
-        @pl.when(c == 13)
-        def _():
-            for k in range(2):
-                for step in (1, 3):
-                    g_copy(k, step).wait_recv()
-                for j in (2, 3):
-                    h_copy(k, j, core).start()
-
-        @pl.when(c == BLOCKS - 1)
-        def _():
-            for k in range(2):
-                f_copy(k, 1).wait_recv()
-                h_copy(k, 1, core).start()
-
         @pl.when(c == 6)
         def _():
             arrived(3)
             for step in (1, 3, 2):
-                w_copy(w_all.at[on(1 - plane, 0), rows_of(core)], on(1 - plane, 0), 3 + RING - step, on(plane, step)).start()
-
-        @pl.when(c == 10)
+                w_copy(w_all.at[across, rows_of(core)], across, 3 + RING - step, on(plane, step)).start()
+
+        @pl.when(c == 7)
+        def _():
+            for k in range(2):
+                f_copy(k, 1).start()
+
+        @pl.when(c == 11)
         def _():
             for index in (0, 2, 1):
-                arrived(index)
-
-        @pl.when(c == BLOCKS - 1)
-        def _():
-            for index in (4, 6, 5):
                 arrived(index)
 
     def q_copy(step):
@@ -175,7 +160,7 @@
         )
 
     def y_copy(step):
-        slot = {1: 3, 2: 4, 3: 2}[step]
+        slot = {1: 3, 2: 6, 3: 2}[step]
         return remote(
             kv_ref.at[lax.rem(y + step, RING)], kv_in.at[slot], y_send.at[step], kv_recv.at[slot], at(step)
         )
@@ -204,16 +189,25 @@
     def arrive(c):
         d_copy(kv_in.at[c], c).wait_recv()
 
-        @pl.when((c >= 2) & (c <= 4))
-        def _():
-            d_copy(kv_in.at[c], c + 3).start()
+        @pl.when((c == 2) | (c == 3))
+        def _():
+            d_copy(kv_in.at[c], c + 2).start()
             z_copy(kv_in.at[c], 2 * c + 6).start()
 
+        @pl.when(c == 6)
+        def _():
+            d_copy(kv_in.at[c], c + 1).start()
+            z_copy(kv_in.at[c], 14).start()
+
         @pl.when((c >= 8) & (lax.rem(c, 2) == 0))
         def _():
             d_copy(kv_in.at[c], c + 1).start()
 
         pass_on(c)
+
+    def prepare(c):
+        key_rows[c] = kv_in[c, :HD].T
+        values[c, :HD] = kv_in[c, HD:]
 
     def score(c, s, b):
         for lanes in TILES:
@@ -229,44 +223,84 @@
             weights = jnp.exp2(scores[b, :rows, lanes] - new).astype(BF16)
             acc[s, :, lanes] = acc[s, :, lanes] * jnp.exp2(old - new) + dot(values[c], weights)
 
-    order = (0, 1, 3, 2)
-
-    def block(c, first=False):
-        after = jnp.minimum(c + 1, BLOCKS - 1)
-        if first:
-            arrive(after)
-        else:
-            @pl.when(c < BLOCKS - 1)
-            def _():
-                arrive(after)
-
-        key_rows[after] = kv_in[after, :HD].T
-        values[after, :HD] = kv_in[after, HD:]
+    def o_copy(step):
+        return remote(obuf.at[step], out_ref.at[y], o_send.at[step], o_recv.at[RING - step], at(step))
+
+    opening = [(c, s) for s in (0, 1, 3, 2) for c in (0, 1)]
+    last = 12
+    order = (3, 0, 1, 2)
+    score(0, 0, 0)
+    for i, (c, s) in enumerate(opening):
+        if i == 0:
+            arrive(jnp.int32(1))
+            prepare(1)
+        elif i == len(opening) - 1:
+            arrive(jnp.int32(2))
+            prepare(2)
+        after = opening[i + 1] if i + 1 < len(opening) else (2, order[0])
+        if i in (1, 3, 5):
+            q_copy(RING - after[1]).wait_recv()
+        score(*after, (i + 1) % 2)
+        weigh(c, s, i % 2)
+
+    def body(c, carry):
+        arrive(c + 1)
+
+        @pl.when(c == last - 1)
+        def _():
+            arrive(jnp.int32(14))
+
+        prepare(c + 1)
         for i, s in enumerate(order):
-            if first and i < 3:
-                q_copy(RING - order[i + 1]).wait_recv()
             if i < 3:
                 score(c, order[i + 1], 1 - i % 2)
             else:
-                score(after, order[0], 0)
+                score(c + 1, order[0], 0)
             weigh(c, s, i % 2)
-
-    score(0, order[0], 0)
-    block(jnp.int32(0), True)
-
-    def body(c, carry):
-        block(c)
         return carry
 
-    lax.fori_loop(1, BLOCKS, body, 0)
-
-    def o_copy(step):
-        return remote(obuf.at[step], out_ref.at[y], o_send.at[step], o_recv.at[RING - step], at(step))
-
-    for s in (2, 1, 3):
-        obuf[s, :, :rows] = (acc[s, :HD] / acc[s, HD : HD + 1]).astype(BF16)
-        o_copy(s).start()
-    out_ref[y, :, :rows] = (acc[0, :HD] / acc[0, HD : HD + 1]).astype(BF16)
+    lax.fori_loop(2, last, body, 0)
+
+    arrive(jnp.int32(13))
+    arrive(jnp.int32(15))
+    for k in range(2):
+        for step in (1, 3):
+            g_copy(k, step).wait_recv()
+        for j in (2, 3):
+            h_copy(k, j, core).start()
+    for c in range(last + 1, BLOCKS):
+        prepare(c)
+
+    def close(i, carry):
+        s = RING - 1 - i
+        for k in range(RING):
+            if k < RING - 1:
+                score(last + k + 1, s, 1 - k % 2)
+            else:
+                score(last, jnp.maximum(s - 1, 0), 0)
+            weigh(last + k, s, k % 2)
+        result = (acc[s, :HD] / acc[s, HD : HD + 1]).astype(BF16)
+
+        @pl.when(s > 0)
+        def _():
+            obuf[s, :, :rows] = result
+            o_copy(s).start()
+
+        @pl.when(s == 0)
+        def _():
+            out_ref[y, :, :rows] = result
+
+        @pl.when(s == 1)
+        def _():
+            for k in range(2):
+                f_copy(k, 1).wait_recv()
+                h_copy(k, 1, core).start()
+            for index in (4, 6, 5):
+                arrived(index)
+
+        return carry
+
+    lax.fori_loop(0, RING, close, 0)
     out_ref[y, :, rows:] = jnp.zeros((HD, out_ref.shape[2] - rows), BF16)
 
     def o_wait(step):
@@ -280,7 +314,7 @@
         o_copy(step).wait_send()
     for slot in (8, 10, 12, 14):
         z_copy(own, slot).wait_send()
-    for slot in (1, 5, 6, 7, 9, 11, 13, 15):
+    for slot in (1, 4, 5, 7, 9, 11, 13, 15):
         d_copy(own, slot).wait_send()
     for index in range(7):
         w_copy(w_mine, tensor, index, tensor).wait_send()
@@ -329,7 +363,7 @@
         ],
         cost_estimate=pl.CostEstimate(flops=40 * 10**9, bytes_accessed=8 << 20, transcendentals=0),
         compiler_params=pltpu.CompilerParams(
-            vmem_limit_bytes=40 << 20, collective_id=0, has_side_effects=True
+            vmem_limit_bytes=62 << 20, collective_id=0, has_side_effects=True
         ),
     )(query, kv, w_out, w_up, w_down)
 

time: 118 us -> 115 us (0.975)
  Pallas kernels: 105 us -> 102 us
  local copies, waits for them, and re-layouts: 7.51 us -> 5.61 us
  other arithmetic: 2.82 us -> 4.34 us
    pallas_call x1, Pallas kernels: 55.6 us -> 52.7 us  [attend(): pl.pallas_call(attend_kernel, in_specs=[vmem, vmem, hbm, hbm, hbm], out_s...]
    unnamed x18 -> x12, local copies, waits for them, and re-layouts: 5.96 us -> 4.06 us
where the time goes in v5:
time: 115 us; the launch traced here: 114 us
  Pallas kernels  102 us (89%)
  local copies, waits for them, and re-layouts  5.61 us (5%)
  other arithmetic  4.34 us (4%)
  matrix products  1.69 us (1%)
    pallas_call x1, Pallas kernels, attend(): pl.pallas_call(attend_kernel, in_specs=[vmem, vmem, hbm, hbm, hbm], out_s...  52.7 us
    pallas_call x1, Pallas kernels, tail(): pl.pallas_call(tail_kernel, in_specs=[vmem, hbm, vmem, hbm, hbm, hbm, hbm...  49.8 us
    unnamed x12, local copies, waits for them, and re-layouts  4.06 us

profile of v5, /device:TPU:0, one launch (start us, length us, event | category | flops | bytes accessed | tf_op | source)
XLA Modules:
  0.0 114.2 jit_solution(15680451563778999511)
XLA Ops:
  0.0 0.0 copy-start
  0.0 0.0 copy-start.1
  0.0 0.0 copy-start.4
  0.0 1.5 %copy-done = bf16[1536,3,192]{0,2,1:T(8,128)(2,1)S(1)} copy-done((bf16[1536,3,192]{0,2,1:T(8,128)(2,1)S(1)}, bf16[1536,3,192]{0,2,1:T(8,128)(2,1)}, u32[]{:S(2)}) %copy-start) | copy-done | bytes 1769496
  1.5 0.0 copy-start.5
  1.5 2.0 %convert_reduce_fusion = f32[720]{0:T(1024)S(1)} fusion(bf16[720,1536]{1,0:T(8,128)(2,1)} %tokens_hbm.1), kind=kLoop, calls=%fused_computation.1 | loop fusion | flops 2211120 | bytes 2214720 | tf_op jit(solution)/shard_map/reduce_sum | solution.py:20
  3.5 0.0 copy-done.1
  3.5 0.7 fusion.2
  4.2 0.0 copy-done.4
  4.2 0.0 copy-done.5
  4.3 1.7 %fusion.15 = (bf16[576,720]{1,0:T(8,128)(2,1)S(1)}, f32[576,720]{1,0:T(8,128)S(1)}) fusion(bf16[1536,576]{0,1:T(8,128)(2,1)S(1)} %bitcast.11, bf16[720,1536]{1,0:T(8,128)(2,1)S(1)} %copy-done.1, f32[1536]{0:T(1024)S(1)} %copy-done.5, f32[720]{0:T(1024)S(1)} %add_rsqrt_fusion, f32[720]{0:T(1024)S(1)} %broadcast_multiply_fusion), kind=kOutput, calls=%fused_computation.18 | convolution fusion | flops 1279964160 | bytes 6481536 | tf_op jit(solution)/shard_map/dot_general | solution.py:613
  6.0 0.9 pad_maximum_fusion.kv_ref
  6.9 0.8 fusion.13
  7.6 52.7 %shard_map.73 = (bf16[4,48,768]{2,1,0:T(8,128)(2,1)}, bf16[8,192,1536]{2,1,0:T(8,128)(2,1)}, bf16[8,192,768]{2,1,0:T(8,128)(2,1)}, bf16[8,96,1536]{2,1,0:T(8,128)(2,1)}) custom-call(bf16[4,48,720]{2,1,0:T(8,128)(2,1)} %bitcast.16, bf16[4,96,720]{2,1,0:T(8,128)(2,1)} %pad_maximum_fusion.kv_ref, bf16[192,1536]{1,0:T(8,128)(2,1)} %w_hbm.1, ...), custom_call_target="tpu_custom_call" | custom-call | flops 40000000000 | bytes 8388608 | tf_op jit(solution)/shard_map/pallas_call | solution.py:341
  60.3 0.0 copy-start.2
  60.3 1.6 %copy-done.2 = bf16[720,1536]{1,0:T(8,128)(2,1)S(1)} copy-done((bf16[720,1536]{1,0:T(8,128)(2,1)S(1)}, bf16[720,1536]{1,0:T(8,128)(2,1)}, u32[]{:S(2)}) %copy-start.2) | copy-done | bytes 2211864
  61.9 0.0 copy-start.3
  61.9 1.0 copy-done.3
  62.9 49.8 %shard_map.74 = bf16[8,96,1536]{2,1,0:T(8,128)(2,1)S(1)} custom-call(bf16[192,768]{1,0:T(8,128)(2,1)S(1)} %bitcast.13, bf16[720,1536]{1,0:T(8,128)(2,1)S(1)} %copy-done.2, f32[1,1536]{1,0:T(1,128)S(1)} %reshape.43.gain_ref, bf16[8,192,1536]{2,1,0:T(8,128)(2,1)} %get-tuple-element.10.w_hbm, bf16[1536,768]{1,0:T(8,128)(2,1)} %up_hbm.1, ...), custom_call_target="tpu_custom_call" | custom-call | flops 60000002048 | bytes 20971520 | tf_op jit(solution)/shard_map/pallas_call | solution.py:580
  112.7 1.5 %slice.24 = bf16[720,1536]{1,0:T(8,128)(2,1)} slice(bf16[768,1536]{1,0:T(8,128)(2,1)S(1)} %bitcast.12), slice={[0:720], [0:1536]} | slice | bytes 4423680 | tf_op jit(solution)/shard_map/slice | solution.py:623
  (4 shorter events, 0.1 us)
Async XLA Ops:
  0.0 1.5 %copy-start = (bf16[1536,3,192]{0,2,1:T(8,128)(2,1)S(1)}, bf16[1536,3,192]{0,2,1:T(8,128)(2,1)}, u32[]{:S(2)}) copy-start(bf16[1536,3,192]{0,2,1:T(8,128)(2,1)} %param.9) | copy-start | bytes 5308420
  0.0 3.5 %copy-start.1 = (bf16[720,1536]{1,0:T(8,128)(2,1)S(1)}, bf16[720,1536]{1,0:T(8,128)(2,1)}, u32[]{:S(2)}) copy-start(bf16[720,1536]{1,0:T(8,128)(2,1)} %tokens_hbm.1) | copy-start | bytes 6635524
  0.0 4.2 %copy-start.4 = (f32[1536]{0:T(1024)S(1)}, f32[1536]{0:T(1024)}, u32[]{:S(2)}) copy-start(f32[1536]{0:T(1024)} %param.11) | copy-start | bytes 18436
  1.5 2.8 %copy-start.5 = (f32[1536]{0:T(1024)S(1)}, f32[1536]{0:T(1024)}, u32[]{:S(2)}) copy-start(f32[1536]{0:T(1024)} %param.8) | copy-start | bytes 18436
  60.3 1.6 %copy-start.2 = (bf16[720,1536]{1,0:T(8,128)(2,1)S(1)}, bf16[720,1536]{1,0:T(8,128)(2,1)}, u32[]{:S(2)}) copy-start(bf16[720,1536]{1,0:T(8,128)(2,1)} %tokens_hbm.1) | copy-start | bytes 6635524
  61.9 1.0 copy-start.3

commit v6 on v5

--- a/solution.py
+++ b/solution.py
@@ -34,11 +34,18 @@
 
 
 def attend_kernel(
-    q_ref, kv_ref, w_hbm, up_ref, down_ref, out_ref, w_all, up_all, down_all, w_ref, q_in, kv_in, key_rows, values, acc, peak, scores, obuf,
+    tokens_hbm, gain_ref, w_qkv_hbm, w_hbm, up_ref, down_ref, out_ref, w_all, up_all, down_all,
+    tokens, w_qkv, q_ref, kv_ref, w_ref, q_in, kv_in, key_rows, values, acc, peak, scores, obuf,
     q_send, q_recv, y_send, z_send, d_send, kv_recv, o_send, o_recv, w_send, w_recv, t_send, t_recv, w_own,
-    f_send, f_recv, g_send, g_recv, h_send, h_recv,
+    f_send, f_recv, g_send, g_recv, h_send, h_recv, load_sem,
 ):
     rows = q_ref.shape[2]
+    loads = (
+        pltpu.make_async_copy(tokens_hbm, tokens, load_sem.at[0]),
+        pltpu.make_async_copy(w_qkv_hbm, w_qkv, load_sem.at[1]),
+    )
+    for load in loads:
+        load.start()
     me = lax.axis_index("seq")
     half, y, core = me // (2 * RING), (me // 2) % RING, me % 2
 
@@ -67,10 +74,24 @@
     values[:, HD:, :] = jnp.ones((BLOCKS, values.shape[1] - HD, rows), BF16)
     acc[...] = jnp.zeros_like(acc)
     peak[...] = jnp.full_like(peak, -1e30)
-    q_in[0] = q_ref[y]
     obuf[:, :, rows:] = jnp.zeros((RING, HD, obuf.shape[2] - rows), BF16)
-    key_rows[0] = kv_ref[y, :HD].T
-    values[0, :HD] = kv_ref[y, HD:]
+    loads[0].wait()
+    some = rows // 5
+
+    def norm(i, carry):
+        where = pl.ds(pl.multiple_of(i * some, some), some)
+        tokens[where] = layer_norm(tokens[where].astype(F32), gain_ref[...]).astype(BF16)
+        return carry
+
+    lax.fori_loop(0, 5, norm, 0)
+    loads[1].wait()
+    for lanes in TILES:
+        found = lax.dot_general(
+            w_qkv[...], tokens[lanes], (((1,), (1,)), ((), ())), preferred_element_type=F32
+        ).reshape(3, RING, HD, lanes.stop - lanes.start)
+        q_ref[:, :, lanes] = (found[0] * (LOG2E / HD**0.5)).astype(BF16)
+        kv_ref[:, :HD, lanes] = found[1].astype(BF16)
+        kv_ref[:, HD:, lanes] = found[2].astype(BF16)
     pl.semaphore_wait(barrier, len(peers) + len(friends) + 1)
 
     pieces = 2 * RING
@@ -185,6 +206,10 @@
     w_copy(w_mine, tensor, 3, across).start()
     for step in (1, 3, 2):
         w_copy(w_mine, tensor, RING - step - 1, on(plane, step)).start()
+
+    q_in[0] = q_ref[y]
+    key_rows[0] = kv_ref[y, :HD].T
+    values[0, :HD] = kv_ref[y, HD:]
 
     def arrive(c):
         d_copy(kv_in.at[c], c).wait_recv()
@@ -250,12 +275,13 @@
         def _():
             arrive(jnp.int32(14))
 
-        prepare(c + 1)
         for i, s in enumerate(order):
             if i < 3:
                 score(c, order[i + 1], 1 - i % 2)
             else:
                 score(c + 1, order[0], 0)
+            if i == 2:
+                prepare(c + 1)
             weigh(c, s, i % 2)
         return carry
 
@@ -333,14 +359,15 @@
         o_wait(step).wait_recv()
 
 
-def attend(query, kv, w_out, w_up, w_down, padded, n_tensor):
-    heads, width, rows = query.shape
+def attend(tokens, gain, w_qkv, w_out, w_up, w_down, padded, n_tensor):
+    rows = tokens.shape[0]
+    heads, width = RING, HD
     dma = lambda n: pltpu.SemaphoreType.DMA((n,))
     vmem = pl.BlockSpec(memory_space=pltpu.VMEM)
     hbm = pl.BlockSpec(memory_space=pltpu.HBM)
     return pl.pallas_call(
         attend_kernel,
-        in_specs=[vmem, vmem, hbm, hbm, hbm],
+        in_specs=[hbm, vmem, hbm, hbm, hbm, hbm],
         out_specs=[vmem, hbm, hbm, hbm],
         out_shape=[
             jax.ShapeDtypeStruct((heads, width, padded), BF16),
@@ -348,6 +375,10 @@
             *(jax.ShapeDtypeStruct((2 * RING, w.shape[0] // (2 * RING), w.shape[1]), BF16) for w in (w_up, w_down)),
         ],
         scratch_shapes=[
+            pltpu.VMEM(tokens.shape, BF16),
+            pltpu.VMEM(w_qkv.shape, BF16),
+            pltpu.VMEM((heads, width, rows), BF16),
+            pltpu.VMEM((heads, 2 * width, rows), BF16),
             pltpu.VMEM(w_out.shape, BF16),
             pltpu.VMEM((heads, width, rows), BF16),
             pltpu.VMEM((BLOCKS, 2 * width, rows), BF16),
@@ -359,13 +390,13 @@
             pltpu.VMEM((heads, width, padded), BF16),
             dma(RING), dma(RING), dma(RING), dma(BLOCKS), dma(BLOCKS), dma(BLOCKS), dma(RING), dma(RING),
             dma(7), dma(7), dma(7), dma(7), dma(2),
-            dma(4), dma(4), dma(4), dma(4), dma(8), dma(8),
+            dma(4), dma(4), dma(4), dma(4), dma(8), dma(8), dma(2),
         ],
         cost_estimate=pl.CostEstimate(flops=40 * 10**9, bytes_accessed=8 << 20, transcendentals=0),
         compiler_params=pltpu.CompilerParams(
             vmem_limit_bytes=62 << 20, collective_id=0, has_side_effects=True
         ),
-    )(query, kv, w_out, w_up, w_down)
+    )(tokens, gain, w_qkv, w_out, w_up, w_down)
 
 
 class Tensor:
@@ -597,25 +628,20 @@
             dma(9), dma(9), dma(6), dma(6), dma(9), dma(9), dma(6),
         ],
         cost_estimate=pl.CostEstimate(flops=60 * 10**9, bytes_accessed=20 << 20, transcendentals=0),
-        compiler_params=pltpu.CompilerParams(vmem_limit_bytes=48 << 20, collective_id=1, has_side_effects=True),
+        compiler_params=pltpu.CompilerParams(vmem_limit_bytes=62 << 20, collective_id=1, has_side_effects=True),
     )(heads, tokens, gain, w_out, up, up_pair, down, down_pair)
 
 
 def per_device(n_seq, n_tensor, tokens, norm_gain, w_qkv, w_out, post_gain, w_up, w_down):
     rows, model = tokens.shape
     span = w_qkv.shape[2]
-    heads = span // HD
     part = -(-rows // (16 * n_tensor)) * 16
     padded = n_tensor * part
 
-    base = tokens.astype(F32)
-    normed = layer_norm(base, norm_gain).astype(BF16)
-    qkv = lax.dot_general(
-        w_qkv.reshape(model, -1), normed, (((0,), (1,)), ((), ())), preferred_element_type=F32
-    ).reshape(3, heads, HD, rows)
-    query = (qkv[0] * (LOG2E / HD**0.5)).astype(BF16)
-    kv = jnp.concatenate([qkv[1], qkv[2]], axis=1).astype(BF16)
-    attended, w_out_all, up_pair, down_pair = attend(query, kv, w_out, w_up, w_down, padded, n_tensor)
+    attended, w_out_all, up_pair, down_pair = attend(
+        tokens, norm_gain.reshape(1, model), w_qkv.transpose(1, 2, 0).reshape(3 * span, model),
+        w_out, w_up, w_down, padded, n_tensor,
+    )
     out = tail(
         attended.reshape(span, padded), tokens, post_gain.reshape(1, model), w_out_all,
         w_up, up_pair.reshape(w_up.shape), w_down, down_pair.reshape(w_down.shape), part,

time: 115 us -> 114 us (level)
  Pallas kernels: 102 us -> 108 us
  other arithmetic: 4.34 us -> 0 us
  matrix products: 1.69 us -> 0 us
    unnamed x12 -> x0, local copies, waits for them, and re-layouts: 4.06 us -> none
    pallas_call x1, Pallas kernels: 49.8 us -> 53.1 us  [tail(): pl.pallas_call(tail_kernel, in_specs=[vmem, hbm, vmem, hbm, hbm, hbm, hbm...]
    reduce_sum x2 -> x0, other arithmetic: 2.7 us -> none  [the longest x1 1.99 us: layer_norm(): mean = jnp.mean(values, axis=-1, keepdims=True)]
    pallas_call x1, Pallas kernels: 52.7 us -> 54.5 us  [attend(): pl.pallas_call(attend_kernel, in_specs=[hbm, vmem, hbm, hbm, hbm, hbm], o...]
    dot_general x1 -> x0, matrix products: 1.69 us -> none  [per_device(): lax.dot_general(w_qkv.reshape(model, -1), normed, (((0,), (1,)), ((), ())...]
    slice x1, local copies, waits for them, and re-layouts: 1.5 us -> 3.12 us  [per_device(): return out.reshape(padded, model)[:rows]]
    reshape x0 -> x1, local copies, waits for them, and re-layouts: none -> 1.29 us  [per_device(): norm_gain.reshape(1, model)]
    reshape x1, local copies, waits for them, and re-layouts: 0.01 us -> 1.29 us  [per_device(): post_gain.reshape(1, model)]
where the time goes in v6:
time: 114 us; the launch traced here: 113 us
  Pallas kernels  108 us (95%)
  local copies, waits for them, and re-layouts  5.71 us (5%)
    pallas_call x1, Pallas kernels, attend(): pl.pallas_call(attend_kernel, in_specs=[hbm, vmem, hbm, hbm, hbm, hbm], o...  54.5 us
    pallas_call x1, Pallas kernels, tail(): pl.pallas_call(tail_kernel, in_specs=[vmem, hbm, vmem, hbm, hbm, hbm, hbm...  53.1 us
    slice x1, local copies, waits for them, and re-layouts, per_device(): return out.reshape(padded, model)[:rows]  3.12 us

profile of v6, /device:TPU:0, one launch (start us, length us, event | category | flops | bytes accessed | tf_op | source)
XLA Modules:
  0.0 113.3 jit_solution(9993838480499530742)
XLA Ops:
  0.0 1.3 %reshape.21.gain_ref = f32[1,1536]{1,0:T(1,128)} reshape(f32[1536]{0:T(1024)} %param.8) | data formatting | bytes 12288 | tf_op jit(solution)/shard_map/reshape | solution.py:642
  1.3 1.3 %reshape.24.gain_ref = f32[1,1536]{1,0:T(1,128)} reshape(f32[1536]{0:T(1024)} %param.11) | data formatting | bytes 12288 | tf_op jit(solution)/shard_map/reshape | solution.py:646
  2.6 54.5 %shard_map.73 = (bf16[4,48,768]{2,1,0:T(8,128)(2,1)}, bf16[8,192,1536]{2,1,0:T(8,128)(2,1)}, bf16[8,192,768]{2,1,0:T(8,128)(2,1)}, bf16[8,96,1536]{2,1,0:T(8,128)(2,1)}) custom-call(bf16[720,1536]{1,0:T(8,128)(2,1)} %tokens_hbm.3, f32[1,1536]{1,0:T(1,128)} %reshape.21.gain_ref, bf16[576,1536]{1,0:T(8,128)(2,1)} %bitcast.8, bf16[192,1536]{1,0:T(8,128)(2,1)} %w_hbm.1, ...), custom_call_target="tpu_custom_call" | custom-call | flops 40000000000 | bytes 8388608 | tf_op jit(solution)/shard_map/pallas_call | solution.py:368
  57.1 53.1 %shard_map.74 = bf16[8,96,1536]{2,1,0:T(8,128)(2,1)} custom-call(bf16[192,768]{1,0:T(8,128)(2,1)} %bitcast.11, bf16[720,1536]{1,0:T(8,128)(2,1)} %tokens_hbm.3, f32[1,1536]{1,0:T(1,128)} %reshape.24.gain_ref, bf16[8,192,1536]{2,1,0:T(8,128)(2,1)} %get-tuple-element.10.w_hbm, bf16[1536,768]{1,0:T(8,128)(2,1)} %up_hbm.1, bf16[1536,768]{1,0:T(8,128)(2,1)} %bitcast.9, ...), custom_call_target="tpu_custom_call" | custom-call | flops 60000002048 | bytes 20971520 | tf_op jit(solution)/shard_map/pallas_call | solution.py:611
  110.2 3.1 %slice.4 = bf16[720,1536]{1,0:T(8,128)(2,1)} slice(bf16[768,1536]{1,0:T(8,128)(2,1)} %bitcast.7), slice={[0:720], [0:1536]} | slice | bytes 4423680 | tf_op jit(solution)/shard_map/slice | solution.py:649

commit v7 on v6

--- a/solution.py
+++ b/solution.py
@@ -12,6 +12,7 @@
 F32 = jnp.float32
 BF16 = jnp.bfloat16
 RING = 4
+GRANT = 61 << 20
 BLOCKS = 16
 TILES = (slice(0, 256), slice(256, 512), slice(512, 720))
 
@@ -34,10 +35,10 @@
 
 
 def attend_kernel(
-    tokens_hbm, gain_ref, w_qkv_hbm, w_hbm, up_ref, down_ref, out_ref, w_all, up_all, down_all,
-    tokens, w_qkv, q_ref, kv_ref, w_ref, q_in, kv_in, key_rows, values, acc, peak, scores, obuf,
+    tokens_hbm, gain_ref, w_qkv_hbm, w_hbm, post_gain_ref, up_hbm, down_hbm, out_ref,
+    heads_ref, w_all, up, down, tokens, w_qkv, q_ref, kv_ref, q_in, kv_in, key_rows, values, acc, peak, scores, obuf,
     q_send, q_recv, y_send, z_send, d_send, kv_recv, o_send, o_recv, w_send, w_recv, t_send, t_recv, w_own,
-    f_send, f_recv, g_send, g_recv, h_send, h_recv, load_sem,
+    f_send, f_recv, g_send, g_recv, h_send, h_recv, load_sem, *tail_scratch,
 ):
     rows = q_ref.shape[2]
     loads = (
@@ -69,7 +70,7 @@
         pl.semaphore_signal(barrier, inc=1, device_id={"tensor": friend}, device_id_type=MESH)
     across = on(1 - plane, 0)
     pl.semaphore_signal(barrier, inc=1, device_id={"seq": far, "tensor": across}, device_id_type=MESH)
-    w_load = pltpu.make_async_copy(w_hbm, w_ref, w_own.at[0])
+    w_load = pltpu.make_async_copy(w_hbm, w_all.at[tensor], w_own.at[0])
     w_load.start()
     values[:, HD:, :] = jnp.ones((BLOCKS, values.shape[1] - HD, rows), BF16)
     acc[...] = jnp.zeros_like(acc)
@@ -80,7 +81,7 @@
 
     def norm(i, carry):
         where = pl.ds(pl.multiple_of(i * some, some), some)
-        tokens[where] = layer_norm(tokens[where].astype(F32), gain_ref[...]).astype(BF16)
+        tokens[where] = layer_norm(tokens[where].astype(F32), gain_ref[...].reshape(1, -1)).astype(BF16)
         return carry
 
     lax.fori_loop(0, 5, norm, 0)
@@ -95,36 +96,38 @@
     pl.semaphore_wait(barrier, len(peers) + len(friends) + 1)
 
     pieces = 2 * RING
-    both = ((up_ref, up_all), (down_ref, down_all))
+    both = ((up_hbm, up), (down_hbm, down))
+
+    def spot(k, number):
+        size = both[k][0].shape[0] // pieces
+        return both[k][1].at[1, pl.ds(pl.multiple_of(number * size, size), size)]
 
     def piece(j, which):
         return lax.rem(y + (0, 2, 1, 3)[j], RING) * 2 + which
 
     def f_copy(k, j):
-        ref, whole = both[k]
+        ref = both[k][0]
         size = ref.shape[0] // pieces
         number = piece(j, core)
         src = ref.at[pl.ds(pl.multiple_of(number * size, size), size)]
         device = {"tensor": across} if k == 0 else {"seq": far, "tensor": across}
         return pltpu.make_async_remote_copy(
-            src_ref=src, dst_ref=whole.at[number], send_sem=f_send.at[2 * k + j], recv_sem=f_recv.at[2 * k + j],
+            src_ref=src, dst_ref=spot(k, number), send_sem=f_send.at[2 * k + j], recv_sem=f_recv.at[2 * k + j],
             device_id=device, device_id_type=MESH,
         )
 
     def g_copy(k, step):
-        whole = both[k][1]
         number = piece(0, core)
         i = 2 * k + step // 2
         j = 2 * k + 1 - step // 2
-        return remote(whole.at[number], whole.at[number], g_send.at[i], g_recv.at[j], at(step))
+        return remote(spot(k, number), spot(k, number), g_send.at[i], g_recv.at[j], at(step))
 
     def h_copy(k, j, which):
-        whole = both[k][1]
         number = piece(j, which)
         i = 4 * k + j
-        return remote(whole.at[number], whole.at[number], h_send.at[i], h_recv.at[i], twin)
-
-    cut = w_ref.shape[0] // 2
+        return remote(spot(k, number), spot(k, number), h_send.at[i], h_recv.at[i], twin)
+
+    cut = w_hbm.shape[0] // 2
     rows_of = lambda which: pl.ds(pl.multiple_of(which * cut, cut), cut)
 
     def w_copy(src, owner, index, friend):
@@ -143,8 +146,7 @@
             w_all.at[owner, rows_of(which)], w_all.at[owner, rows_of(which)], t_send.at[index], t_recv.at[index], twin
         )
 
-    w_mine = w_ref.at[rows_of(core)]
-    w_local = pltpu.make_async_copy(w_ref, w_all.at[tensor], w_own.at[1])
+    w_mine = w_all.at[tensor, rows_of(core)]
 
     def arrived(index):
         w_copy(w_mine, tensor, index, tensor).wait_recv()
@@ -202,7 +204,6 @@
     f_copy(0, 0).start()
     f_copy(1, 0).start()
     w_load.wait()
-    w_local.start()
     w_copy(w_mine, tensor, 3, across).start()
     for step in (1, 3, 2):
         w_copy(w_mine, tensor, RING - step - 1, on(plane, step)).start()
@@ -248,8 +249,10 @@
             weights = jnp.exp2(scores[b, :rows, lanes] - new).astype(BF16)
             acc[s, :, lanes] = acc[s, :, lanes] * jnp.exp2(old - new) + dot(values[c], weights)
 
+    head = lambda which: pl.ds(pl.multiple_of(which * HD, HD), HD)
+
     def o_copy(step):
-        return remote(obuf.at[step], out_ref.at[y], o_send.at[step], o_recv.at[RING - step], at(step))
+        return remote(obuf.at[step], heads_ref.at[head(y)], o_send.at[step], o_recv.at[RING - step], at(step))
 
     opening = [(c, s) for s in (0, 1, 3, 2) for c in (0, 1)]
     last = 12
@@ -314,7 +317,7 @@
 
         @pl.when(s == 0)
         def _():
-            out_ref[y, :, :rows] = result
+            heads_ref[head(y), :rows] = result
 
         @pl.when(s == 1)
         def _():
@@ -327,11 +330,11 @@
         return carry
 
     lax.fori_loop(0, RING, close, 0)
-    out_ref[y, :, rows:] = jnp.zeros((HD, out_ref.shape[2] - rows), BF16)
+    heads_ref[head(y), rows:] = jnp.zeros((HD, heads_ref.shape[1] - rows), BF16)
 
     def o_wait(step):
         return remote(
-            obuf.at[step], out_ref.at[lax.rem(y + step, RING)], o_send.at[step], o_recv.at[step], at(step)
+            obuf.at[step], heads_ref.at[head(lax.rem(y + step, RING))], o_send.at[step], o_recv.at[step], at(step)
         )
 
     for step in (1, 2, 3):
@@ -342,11 +345,25 @@
         z_copy(own, slot).wait_send()
     for slot in (1, 4, 5, 7, 9, 11, 13, 15):
         d_copy(own, slot).wait_send()
+    for step in (1, 3, 2):
+        o_wait(step).wait_recv()
+
+    def weights_out():
+        for index in range(7):
+            t_copy(index, 1 - core).wait_recv()
+
+    def weights_in():
+        for k in range(2):
+            for j in range(4):
+                h_copy(k, j, 1 - core).wait_recv()
+
+    tail_kernel(
+        heads_ref, tokens_hbm, post_gain_ref, up_hbm, down_hbm, out_ref, w_all, up, down,
+        weights_out, weights_in, *tail_scratch,
+    )
     for index in range(7):
         w_copy(w_mine, tensor, index, tensor).wait_send()
         t_copy(index, core).wait_send()
-        t_copy(index, 1 - core).wait_recv()
-    w_local.wait()
     for k in range(2):
         for j in range(2):
             f_copy(k, j).wait_send()
@@ -354,49 +371,6 @@
             g_copy(k, step).wait_send()
         for j in range(4):
             h_copy(k, j, core).wait_send()
-            h_copy(k, j, 1 - core).wait_recv()
-    for step in (1, 3, 2):
-        o_wait(step).wait_recv()
-
-
-def attend(tokens, gain, w_qkv, w_out, w_up, w_down, padded, n_tensor):
-    rows = tokens.shape[0]
-    heads, width = RING, HD
-    dma = lambda n: pltpu.SemaphoreType.DMA((n,))
-    vmem = pl.BlockSpec(memory_space=pltpu.VMEM)
-    hbm = pl.BlockSpec(memory_space=pltpu.HBM)
-    return pl.pallas_call(
-        attend_kernel,
-        in_specs=[hbm, vmem, hbm, hbm, hbm, hbm],
-        out_specs=[vmem, hbm, hbm, hbm],
-        out_shape=[
-            jax.ShapeDtypeStruct((heads, width, padded), BF16),
-            jax.ShapeDtypeStruct((n_tensor, *w_out.shape), BF16),
-            *(jax.ShapeDtypeStruct((2 * RING, w.shape[0] // (2 * RING), w.shape[1]), BF16) for w in (w_up, w_down)),
-        ],
-        scratch_shapes=[
-            pltpu.VMEM(tokens.shape, BF16),
-            pltpu.VMEM(w_qkv.shape, BF16),
-            pltpu.VMEM((heads, width, rows), BF16),
-            pltpu.VMEM((heads, 2 * width, rows), BF16),
-            pltpu.VMEM(w_out.shape, BF16),
-            pltpu.VMEM((heads, width, rows), BF16),
-            pltpu.VMEM((BLOCKS, 2 * width, rows), BF16),
-            pltpu.VMEM((BLOCKS, rows, width), BF16),
-            pltpu.VMEM((BLOCKS, width + 16, rows), BF16),
-            pltpu.VMEM((heads, width + 16, rows), F32),
-            pltpu.VMEM((heads, 1, rows), F32),
-            pltpu.VMEM((2, rows + 8, rows), F32),
-            pltpu.VMEM((heads, width, padded), BF16),
-            dma(RING), dma(RING), dma(RING), dma(BLOCKS), dma(BLOCKS), dma(BLOCKS), dma(RING), dma(RING),
-            dma(7), dma(7), dma(7), dma(7), dma(2),
-            dma(4), dma(4), dma(4), dma(4), dma(8), dma(8), dma(2),
-        ],
-        cost_estimate=pl.CostEstimate(flops=40 * 10**9, bytes_accessed=8 << 20, transcendentals=0),
-        compiler_params=pltpu.CompilerParams(
-            vmem_limit_bytes=62 << 20, collective_id=0, has_side_effects=True
-        ),
-    )(tokens, gain, w_qkv, w_out, w_up, w_down)
 
 
 class Tensor:
@@ -462,8 +436,8 @@
 
 
 def tail_kernel(
-    heads_ref, tokens_hbm, gain_ref, w_hbm, up_hbm, up_pair_hbm, down_hbm, down_pair_hbm, out_ref,
-    heads, w_out, up, down, tokens, mixed, term, own, half_in, edge_in, edge_sum,
+    heads_ref, tokens_hbm, gain_ref, up_hbm, down_hbm, out_ref, w_out, up, down, weights_out, weights_in,
+    heads, tokens, mixed, term, own, half_in, edge_in, edge_sum,
     a_send, a_recv, s_send, s_recv, g_send, g_recv, load_sem,
 ):
     t = Tensor()
@@ -472,14 +446,11 @@
     there = 1 - t.plane
     valid = tokens_hbm.shape[0] - half
     loads = [
-        pltpu.make_async_copy(w_hbm, w_out, load_sem.at[0]),
-        pltpu.make_async_copy(up_hbm, up.at[0], load_sem.at[1]),
-        pltpu.make_async_copy(up_pair_hbm, up.at[1], load_sem.at[2]),
-        pltpu.make_async_copy(down_hbm, down.at[0], load_sem.at[3]),
-        pltpu.make_async_copy(down_pair_hbm, down.at[1], load_sem.at[4]),
+        pltpu.make_async_copy(up_hbm, up.at[0], load_sem.at[0]),
+        pltpu.make_async_copy(down_hbm, down.at[0], load_sem.at[1]),
     ]
-    first = pltpu.make_async_copy(tokens_hbm.at[pl.ds(0, half)], tokens, load_sem.at[5])
-    second = pltpu.make_async_copy(tokens_hbm.at[pl.ds(half, valid)], tokens.at[pl.ds(0, valid)], load_sem.at[5])
+    first = pltpu.make_async_copy(tokens_hbm.at[pl.ds(0, half)], tokens, load_sem.at[2])
+    second = pltpu.make_async_copy(tokens_hbm.at[pl.ds(half, valid)], tokens.at[pl.ds(0, valid)], load_sem.at[2])
 
     @pl.when(t.plane == 0)
     def _():
@@ -492,7 +463,6 @@
 
     for load in loads:
         load.start()
-    t.meet()
 
     cut = heads_ref.shape[0] // 2
     lo, hi = pl.ds(0, cut), pl.ds(cut, cut)
@@ -527,7 +497,7 @@
         second.wait()
 
     mixed[...] = tokens[...].astype(F32)
-    loads[0].wait()
+    weights_out()
 
     def group(i, carry):
         for when, waits, starts in (
@@ -554,8 +524,9 @@
         return carry
 
     lax.fori_loop(0, 2 * RING, group, 0)
-    for load in loads[1:]:
+    for load in loads:
         load.wait()
+    weights_in()
 
     cut = part // 2
     lo, hi = pl.ds(0, cut), pl.ds(cut, cut)
@@ -574,7 +545,7 @@
 
     def feed(i, carry):
         b = lax.rem(t.x + 2 + 3 * i * (i + 1) // 2, RING)
-        post = layer_norm(mixed[rows_of(b)], gain_ref[...]).astype(BF16)
+        post = layer_norm(mixed[rows_of(b)], gain_ref[...].reshape(1, -1)).astype(BF16)
         wide = lambda k: jax.nn.gelu(dot(post, up[k]), approximate=True).astype(BF16)
         term[b] = (dot(wide(0), down[0]) + dot(wide(1), down[1])).astype(BF16)
         for when, starts in ((0, (half_left, half_right)), (1, (edge_right,)), (2, (edge_left,))):
@@ -602,51 +573,65 @@
     gather(t, own, out_ref, cut, g_send, g_recv)
 
 
-def tail(heads, tokens, gain, w_out, up, up_pair, down, down_pair, part):
-    n_tensor, span, model = w_out.shape
-    half = RING * part
+def layer(tokens, gain, w_qkv, w_out, post_gain, up, down, part, n_tensor):
+    rows, model = tokens.shape
+    half, padded = RING * part, n_tensor * part
+    span = w_out.shape[0]
     dma = lambda n: pltpu.SemaphoreType.DMA((n,))
     vmem = pl.BlockSpec(memory_space=pltpu.VMEM)
     hbm = pl.BlockSpec(memory_space=pltpu.HBM)
+    held = lambda *shape: pltpu.VMEM(shape, BF16)
     return pl.pallas_call(
-        tail_kernel,
-        in_specs=[vmem, hbm, vmem, hbm, hbm, hbm, hbm, hbm],
+        attend_kernel,
+        in_specs=[hbm, vmem, hbm, hbm, vmem, hbm, hbm],
         out_specs=vmem,
         out_shape=jax.ShapeDtypeStruct((n_tensor, part, model), BF16),
         scratch_shapes=[
-            pltpu.VMEM((n_tensor, span, half), BF16),
-            pltpu.VMEM(w_out.shape, BF16),
-            pltpu.VMEM((2, *up.shape), BF16),
-            pltpu.VMEM((2, *down.shape), BF16),
-            pltpu.VMEM((half, model), BF16),
+            held(span, padded),
+            held(n_tensor, *w_out.shape),
+            held(2, *up.shape),
+            held(2, *down.shape),
+            held(*tokens.shape),
+            held(*w_qkv.shape),
+            held(RING, HD, rows),
+            held(RING, 2 * HD, rows),
+            held(RING, HD, rows),
+            held(BLOCKS, 2 * HD, rows),
+            held(BLOCKS, rows, HD),
+            held(BLOCKS, HD + 16, rows),
+            pltpu.VMEM((RING, HD + 16, rows), F32),
+            pltpu.VMEM((RING, 1, rows), F32),
+            pltpu.VMEM((2, rows + 8, rows), F32),
+            held(RING, HD, padded),
+            dma(RING), dma(RING), dma(RING), dma(BLOCKS), dma(BLOCKS), dma(BLOCKS), dma(RING), dma(RING),
+            dma(7), dma(7), dma(7), dma(7), dma(1),
+            dma(4), dma(4), dma(4), dma(4), dma(8), dma(8), dma(2),
+            held(n_tensor, span, half),
+            held(half, model),
             pltpu.VMEM((half, model), F32),
-            pltpu.VMEM((RING, part, model), BF16),
-            pltpu.VMEM((part, model), BF16),
-            pltpu.VMEM((2, part // 2, model), BF16),
-            pltpu.VMEM((2, part, model), BF16),
-            pltpu.VMEM((2, part // 2, model), BF16),
-            dma(9), dma(9), dma(6), dma(6), dma(9), dma(9), dma(6),
+            held(RING, part, model),
+            held(part, model),
+            held(2, part // 2, model),
+            held(2, part, model),
+            held(2, part // 2, model),
+            dma(9), dma(9), dma(6), dma(6), dma(9), dma(9), dma(3),
         ],
-        cost_estimate=pl.CostEstimate(flops=60 * 10**9, bytes_accessed=20 << 20, transcendentals=0),
-        compiler_params=pltpu.CompilerParams(vmem_limit_bytes=62 << 20, collective_id=1, has_side_effects=True),
-    )(heads, tokens, gain, w_out, up, up_pair, down, down_pair)
+        cost_estimate=pl.CostEstimate(flops=100 * 10**9, bytes_accessed=30 << 20, transcendentals=0),
+        compiler_params=pltpu.CompilerParams(
+            vmem_limit_bytes=GRANT, collective_id=0, has_side_effects=True
+        ),
+    )(tokens, gain, w_qkv, w_out, post_gain, up, down)
 
 
 def per_device(n_seq, n_tensor, tokens, norm_gain, w_qkv, w_out, post_gain, w_up, w_down):
     rows, model = tokens.shape
     span = w_qkv.shape[2]
     part = -(-rows // (16 * n_tensor)) * 16
-    padded = n_tensor * part
-
-    attended, w_out_all, up_pair, down_pair = attend(
-        tokens, norm_gain.reshape(1, model), w_qkv.transpose(1, 2, 0).reshape(3 * span, model),
-        w_out, w_up, w_down, padded, n_tensor,
+    out = layer(
+        tokens, norm_gain, w_qkv.transpose(1, 2, 0).reshape(3 * span, model), w_out, post_gain, w_up, w_down,
+        part, n_tensor,
     )
-    out = tail(
-        attended.reshape(span, padded), tokens, post_gain.reshape(1, model), w_out_all,
-        w_up, up_pair.reshape(w_up.shape), w_down, down_pair.reshape(w_down.shape), part,
-    )
-    return out.reshape(padded, model)[:rows]
+    return out.reshape(n_tensor * part, model)[:rows]
 
 
 def solution(mesh):

time: 114 us -> 107 us (0.939)
  Pallas kernels: 108 us -> 104 us
  local copies, waits for them, and re-layouts: 5.71 us -> 3.12 us
    pallas_call x2 -> x1, Pallas kernels: 108 us -> 104 us  [layer(): pl.pallas_call(attend_kernel, in_specs=[hbm, vmem, hbm, hbm, vmem, hbm, h...]
    reshape x2 -> x0, local copies, waits for them, and re-layouts: 2.59 us -> none  [the longest x1 1.29 us: per_device(): norm_gain.reshape(1, model)]
where the time goes in v7:
time: 107 us
  Pallas kernels  104 us (97%)
  local copies, waits for them, and re-layouts  3.12 us (3%)
    pallas_call x1, Pallas kernels, layer(): pl.pallas_call(attend_kernel, in_specs=[hbm, vmem, hbm, hbm, vmem, hbm, h...  104 us
    slice x1, local copies, waits for them, and re-layouts, per_device(): return out.reshape(n_tensor * part, model)[:rows]  3.12 us

profile of v7, /device:TPU:0, one launch (start us, length us, event | category | flops | bytes accessed | tf_op | source)
XLA Modules:
  0.0 107.0 jit_solution(1390659811634263436)
XLA Ops:
  0.0 103.9 %shard_map.73 = bf16[8,96,1536]{2,1,0:T(8,128)(2,1)} custom-call(bf16[720,1536]{1,0:T(8,128)(2,1)} %tokens_hbm.1, f32[1536]{0:T(1024)} %gain_ref.1, bf16[576,1536]{1,0:T(8,128)(2,1)} %bitcast.5, bf16[192,1536]{1,0:T(8,128)(2,1)} %w_hbm.1, f32[1536]{0:T(1024)} %post_gain_ref.1, bf16[1536,768]{1,0:T(8,128)(2,1)} %up_hbm.1, bf16[768,1536]{1,0:T(8,128)(2,1)} %down_hbm.1), custom_call_target="tpu_custom_call" | custom-call | flops 99999997952 | bytes 31457280 | tf_op jit(solution)/shard_map/pallas_call | solution.py:584
  103.9 3.1 %slice.4 = bf16[720,1536]{1,0:T(8,128)(2,1)} slice(bf16[768,1536]{1,0:T(8,128)(2,1)} %bitcast.4), slice={[0:720], [0:1536]} | slice | bytes 4423680 | tf_op jit(solution)/shard_map/slice | solution.py:634

commit v8 on v7

--- a/solution.py
+++ b/solution.py
@@ -12,7 +12,7 @@
 F32 = jnp.float32
 BF16 = jnp.bfloat16
 RING = 4
-GRANT = 61 << 20
+GRANT = 58 << 20
 BLOCKS = 16
 TILES = (slice(0, 256), slice(256, 512), slice(512, 720))
 
@@ -195,11 +195,13 @@
         return remote(src, kv_in.at[slot], d_send.at[slot], kv_recv.at[slot], twin)
 
     own = kv_ref.at[y]
-    for step in (1, 3, 2):
+    d_copy(own, 1).start()
+    for step in (1, 3):
         q_copy(step).start()
-    d_copy(own, 1).start()
-    for step in (1, 3, 2):
+    for step in (1, 3):
         y_copy(step).start()
+    q_copy(2).start()
+    y_copy(2).start()
     z_copy(own, 8).start()
     f_copy(0, 0).start()
     f_copy(1, 0).start()
@@ -254,20 +256,19 @@
     def o_copy(step):
         return remote(obuf.at[step], heads_ref.at[head(y)], o_send.at[step], o_recv.at[RING - step], at(step))
 
-    opening = [(c, s) for s in (0, 1, 3, 2) for c in (0, 1)]
+    opening = [(c, s) for s in (0, 1, 3) for c in (0, 1)] + [(2, s) for s in (3, 0, 1)] + [(c, 2) for c in (0, 1, 2)]
     last = 12
     order = (3, 0, 1, 2)
+    met = {0}
     score(0, 0, 0)
     for i, (c, s) in enumerate(opening):
-        if i == 0:
-            arrive(jnp.int32(1))
-            prepare(1)
-        elif i == len(opening) - 1:
-            arrive(jnp.int32(2))
-            prepare(2)
-        after = opening[i + 1] if i + 1 < len(opening) else (2, order[0])
-        if i in (1, 3, 5):
+        after = opening[i + 1] if i + 1 < len(opening) else (3, order[0])
+        if i in (0, 5, len(opening) - 1):
+            arrive(jnp.int32(after[0]))
+            prepare(after[0])
+        if after[1] not in met:
             q_copy(RING - after[1]).wait_recv()
+            met.add(after[1])
         score(*after, (i + 1) % 2)
         weigh(c, s, i % 2)
 
@@ -288,7 +289,7 @@
             weigh(c, s, i % 2)
         return carry
 
-    lax.fori_loop(2, last, body, 0)
+    lax.fori_loop(3, last, body, 0)
 
     arrive(jnp.int32(13))
     arrive(jnp.int32(15))
@@ -400,36 +401,40 @@
 def gather(t, mine, buf, cut, send_sem, recv_sem):
     lo, hi = pl.ds(0, cut), pl.ds(cut, cut)
     copies = {
-        "right": (mine, t.me, None, t.right, 0),
-        "left": (mine, t.me, None, t.left, 1),
-        "pair": (mine, t.me, None, t.pair, 2),
-        "far lo": (None, t.left, lo, t.right, 3),
-        "far hi": (None, t.right, hi, t.left, 4),
-        "over right": (None, t.pair, None, t.right, 5),
-        "over left": (None, t.pair, None, t.left, 6),
-        "pair lo": (None, t.on(t.plane, 2), lo, t.pair, 7),
-        "pair hi": (None, t.on(t.plane, 2), hi, t.pair, 8),
+        "right lo": (mine, t.me, lo, t.right, 0),
+        "left hi": (mine, t.me, hi, t.left, 1),
+        "over lo": (mine, t.me, lo, t.pair, 2),
+        "right hi": (mine, t.me, hi, t.right, 3),
+        "left lo": (mine, t.me, lo, t.left, 4),
+        "over hi": (mine, t.me, hi, t.pair, 5),
+        "far lo": (None, t.left, lo, t.right, 6),
+        "far hi": (None, t.right, hi, t.left, 7),
+        "over right": (None, t.pair, None, t.right, 8),
+        "over left": (None, t.pair, None, t.left, 9),
+        "pair lo": (None, t.on(t.plane, 2), lo, t.pair, 10),
+        "pair hi": (None, t.on(t.plane, 2), hi, t.pair, 11),
     }
 
     def copy(name):
         src, block, part, to, i = copies[name]
         dst = buf.at[block] if part is None else buf.at[block, part]
-        return send(dst if src is None else src, dst, send_sem.at[i], recv_sem.at[i], to)
-
-    for name in ("right", "left", "pair"):
+        return send(dst if src is None else src.at[part], dst, send_sem.at[i], recv_sem.at[i], to)
+
+    for name in ("right lo", "left hi", "over lo", "right hi", "left lo", "over hi"):
         copy(name).start()
-    copy("right").wait_recv()
+    copy("right lo").wait_recv()
     copy("far lo").start()
-    copy("left").wait_recv()
+    copy("left hi").wait_recv()
     copy("far hi").start()
-    copy("pair").wait_recv()
+    copy("over lo").wait_recv()
+    copy("over hi").wait_recv()
     copy("over right").start()
     copy("over left").start()
     copy("far lo").wait_recv()
     copy("pair lo").start()
     copy("far hi").wait_recv()
     copy("pair hi").start()
-    for name in ("over right", "over left", "pair lo", "pair hi"):
+    for name in ("right hi", "left lo", "over right", "over left", "pair lo", "pair hi"):
         copy(name).wait_recv()
     for name in copies:
         copy(name).wait_send()
@@ -472,19 +477,23 @@
         dst = heads.at[block] if rows is None else heads.at[block, rows]
         return send(dst if src is None else src, dst, a_send.at[i], a_recv.at[i], to)
 
-    mine, theirs = heads_ref.at[:, lanes(t.plane)], heads_ref.at[:, lanes(there)]
+    mine = lambda rows: heads_ref.at[rows, lanes(t.plane)]
     copies = [
-        copy(mine, t.me, None, t.right, 0),
-        copy(mine, t.me, None, t.left, 1),
-        copy(theirs, t.me, None, t.pair, 2),
-        copy(None, t.left, lo, t.right, 3),
-        copy(None, t.right, hi, t.left, 4),
-        copy(None, t.pair, None, t.right, 5),
-        copy(None, t.pair, None, t.left, 6),
-        copy(None, t.on(there, 3), lo, t.right, 7),
-        copy(None, t.on(there, 1), hi, t.left, 8),
+        copy(mine(lo), t.me, lo, t.right, 0),
+        copy(mine(hi), t.me, hi, t.left, 1),
+        copy(heads_ref.at[:, lanes(there)], t.me, None, t.pair, 2),
+        copy(mine(hi), t.me, hi, t.right, 3),
+        copy(mine(lo), t.me, lo, t.left, 4),
+        copy(None, t.left, lo, t.right, 5),
+        copy(None, t.right, hi, t.left, 6),
+        copy(None, t.pair, lo, t.right, 7),
+        copy(None, t.pair, hi, t.left, 8),
+        copy(None, t.pair, hi, t.right, 9),
+        copy(None, t.pair, lo, t.left, 10),
+        copy(None, t.on(there, 3), lo, t.right, 11),
+        copy(None, t.on(there, 1), hi, t.left, 12),
     ]
-    for i in (2, 0, 1):
+    for i in (2, 0, 1, 3, 4):
         copies[i].start()
     heads[t.me] = heads_ref[:, lanes(t.plane)]
 
@@ -500,20 +509,21 @@
     weights_out()
 
     def group(i, carry):
-        for when, waits, starts in (
-            (1, (2,), (5, 6)),
-            (2, (0,), (3,)),
-            (3, (1, 5), (4, 7)),
-            (4, (6,), (8,)),
-            (6, (3, 4), ()),
-            (7, (7, 8), ()),
+        for when, pairs in (
+            (1, ((2, (7, 8, 9, 10)),)),
+            (2, ((0, (5,)), (1, (6,)), (3, ()))),
+            (3, ((7, (11,)), (8, (12,)), (9, ()))),
+            (4, ((4, ()),)),
+            (5, ((10, ()),)),
+            (6, ((5, ()), (6, ()))),
+            (7, ((11, ()), (12, ()))),
         ):
             @pl.when(i == when)
             def _():
-                for one in waits:
-                    copies[one].wait_recv()
-                for one in starts:
-                    copies[one].start()
+                for wait, starts in pairs:
+                    copies[wait].wait_recv()
+                    for one in starts:
+                        copies[one].start()
 
         step = lax.rem(3 * (i // 2) * (i // 2 + 1) // 2, RING)
         side = lax.rem(t.plane + i, 2)
@@ -585,7 +595,7 @@
         attend_kernel,
         in_specs=[hbm, vmem, hbm, hbm, vmem, hbm, hbm],
         out_specs=vmem,
-        out_shape=jax.ShapeDtypeStruct((n_tensor, part, model), BF16),
+        out_shape=pltpu.VMEM((n_tensor, part, model), BF16),
         scratch_shapes=[
             held(span, padded),
             held(n_tensor, *w_out.shape),
@@ -614,7 +624,7 @@
             held(2, part // 2, model),
             held(2, part, model),
             held(2, part // 2, model),
-            dma(9), dma(9), dma(6), dma(6), dma(9), dma(9), dma(3),
+            dma(13), dma(13), dma(6), dma(6), dma(12), dma(12), dma(3),
         ],
         cost_estimate=pl.CostEstimate(flops=100 * 10**9, bytes_accessed=30 << 20, transcendentals=0),
         compiler_params=pltpu.CompilerParams(

time: 107 us -> 101 us (0.944)
  Pallas kernels: 104 us -> 99.2 us
  local copies, waits for them, and re-layouts: 3.12 us -> 1.5 us
    pallas_call x1, Pallas kernels: 104 us -> 99.2 us  [layer(): pl.pallas_call(attend_kernel, in_specs=[hbm, vmem, hbm, hbm, vmem, hbm, h...]
    slice x1, local copies, waits for them, and re-layouts: 3.12 us -> 1.5 us  [per_device(): return out.reshape(n_tensor * part, model)[:rows]]
where the time goes in v8:
time: 101 us
  Pallas kernels  99.2 us (98%)
  local copies, waits for them, and re-layouts  1.5 us (1%)
    pallas_call x1, Pallas kernels, layer(): pl.pallas_call(attend_kernel, in_specs=[hbm, vmem, hbm, hbm, vmem, hbm, h...  99.2 us

profile of v8, /device:TPU:0, one launch (start us, length us, event | category | flops | bytes accessed | tf_op | source)
XLA Modules:
  0.0 100.7 jit_solution(14617937941265949667)
XLA Ops:
  0.0 99.2 %shard_map.73 = bf16[8,96,1536]{2,1,0:T(8,128)(2,1)S(1)} custom-call(bf16[720,1536]{1,0:T(8,128)(2,1)} %tokens_hbm.1, f32[1536]{0:T(1024)} %gain_ref.1, bf16[576,1536]{1,0:T(8,128)(2,1)} %bitcast.5, bf16[192,1536]{1,0:T(8,128)(2,1)} %w_hbm.1, f32[1536]{0:T(1024)} %post_gain_ref.1, bf16[1536,768]{1,0:T(8,128)(2,1)} %up_hbm.1, bf16[768,1536]{1,0:T(8,128)(2,1)} %down_hbm.1), custom_call_target="tpu_custom_call" | custom-call | flops 99999997952 | bytes 31457280 | tf_op jit(solution)/shard_map/pallas_call | solution.py:594
  99.2 1.5 %slice.4 = bf16[720,1536]{1,0:T(8,128)(2,1)} slice(bf16[768,1536]{1,0:T(8,128)(2,1)S(1)} %bitcast.4), slice={[0:720], [0:1536]} | slice | bytes 4423680 | tf_op jit(solution)/shard_map/slice | solution.py:644

commit v9 on v8

--- a/solution.py
+++ b/solution.py
@@ -41,10 +41,10 @@
     f_send, f_recv, g_send, g_recv, h_send, h_recv, load_sem, *tail_scratch,
 ):
     rows = q_ref.shape[2]
-    loads = (
-        pltpu.make_async_copy(tokens_hbm, tokens, load_sem.at[0]),
-        pltpu.make_async_copy(w_qkv_hbm, w_qkv, load_sem.at[1]),
-    )
+    loads = [
+        *(pltpu.make_async_copy(tokens_hbm.at[pl.ds(t.start, t.stop - t.start)], tokens.at[pl.ds(t.start, t.stop - t.start)], load_sem.at[i]) for i, t in enumerate(TILES)),
+        pltpu.make_async_copy(w_qkv_hbm, w_qkv, load_sem.at[3]),
+    ]
     for load in loads:
         load.start()
     me = lax.axis_index("seq")
@@ -76,20 +76,19 @@
     acc[...] = jnp.zeros_like(acc)
     peak[...] = jnp.full_like(peak, -1e30)
     obuf[:, :, rows:] = jnp.zeros((RING, HD, obuf.shape[2] - rows), BF16)
+    def norm(where):
+        tokens[where] = layer_norm(tokens[where].astype(F32), gain_ref[...].reshape(1, -1)).astype(BF16)
+
     loads[0].wait()
-    some = rows // 5
-
-    def norm(i, carry):
-        where = pl.ds(pl.multiple_of(i * some, some), some)
-        tokens[where] = layer_norm(tokens[where].astype(F32), gain_ref[...].reshape(1, -1)).astype(BF16)
-        return carry
-
-    lax.fori_loop(0, 5, norm, 0)
-    loads[1].wait()
-    for lanes in TILES:
+    norm(TILES[0])
+    for load in loads[1:]:
+        load.wait()
+    for i, lanes in enumerate(TILES):
         found = lax.dot_general(
             w_qkv[...], tokens[lanes], (((1,), (1,)), ((), ())), preferred_element_type=F32
         ).reshape(3, RING, HD, lanes.stop - lanes.start)
+        if i + 1 < len(TILES):
+            norm(TILES[i + 1])
         q_ref[:, :, lanes] = (found[0] * (LOG2E / HD**0.5)).astype(BF16)
         kv_ref[:, :HD, lanes] = found[1].astype(BF16)
         kv_ref[:, HD:, lanes] = found[2].astype(BF16)
@@ -615,7 +614,7 @@
             held(RING, HD, padded),
             dma(RING), dma(RING), dma(RING), dma(BLOCKS), dma(BLOCKS), dma(BLOCKS), dma(RING), dma(RING),
             dma(7), dma(7), dma(7), dma(7), dma(1),
-            dma(4), dma(4), dma(4), dma(4), dma(8), dma(8), dma(2),
+            dma(4), dma(4), dma(4), dma(4), dma(8), dma(8), dma(4),
             held(n_tensor, span, half),
             held(half, model),
             pltpu.VMEM((half, model), F32),

time: 101 us -> 100 us (0.990)
  no operation moved by 1% of the time
where the time goes in v9:
time: 100 us
  Pallas kernels  98.5 us (98%)
  local copies, waits for them, and re-layouts  1.5 us (2%)
    pallas_call x1, Pallas kernels, layer(): pl.pallas_call(attend_kernel, in_specs=[hbm, vmem, hbm, hbm, vmem, hbm, h...  98.5 us

profile of v9, /device:TPU:0, one launch (start us, length us, event | category | flops | bytes accessed | tf_op | source)
XLA Modules:
  0.0 100.0 jit_solution(4447891084877465811)
XLA Ops:
  0.0 98.5 %shard_map.73 = bf16[8,96,1536]{2,1,0:T(8,128)(2,1)S(1)} custom-call(bf16[720,1536]{1,0:T(8,128)(2,1)} %tokens_hbm.1, f32[1536]{0:T(1024)} %gain_ref.1, bf16[576,1536]{1,0:T(8,128)(2,1)} %bitcast.5, bf16[192,1536]{1,0:T(8,128)(2,1)} %w_hbm.1, f32[1536]{0:T(1024)} %post_gain_ref.1, bf16[1536,768]{1,0:T(8,128)(2,1)} %up_hbm.1, bf16[768,1536]{1,0:T(8,128)(2,1)} %down_hbm.1), custom_call_target="tpu_custom_call" | custom-call | flops 99999997952 | bytes 31457280 | tf_op jit(solution)/shard_map/pallas_call | solution.py:593
  98.5 1.5 %slice.4 = bf16[720,1536]{1,0:T(8,128)(2,1)} slice(bf16[768,1536]{1,0:T(8,128)(2,1)S(1)} %bitcast.4), slice={[0:720], [0:1536]} | slice | bytes 4423680 | tf_op jit(solution)/shard_map/slice | solution.py:643
